TPU v7x, 256 devices: a whole 4x4x8 slice. The times are simulated.
256 devices in a mesh: gx: 4 (over x), gy: 8 (over z_lo, core), gz: 8 (over y, z_hi).
Axes of the slice: x: 4, y: 4, z: 8 (z_hi: 2, z_lo: 4; z = z_hi * 4 + z_lo), core: 2. Of those that a mesh axis runs over, the one named last changes fastest.
Arguments:
- energy: float32 [256, 256, 1024], P(('gz', 'gy', 'gx')), may hold values from -5 to 5
- flow: float32 [4, 256, 256, 1024], P(None, ('gz', 'gy', 'gx')), may hold values from -0.1 to 0.12, as said below
Outputs:
- energy_next: float32 [256, 256, 1024], P('gz', 'gx', 'gy')
- plane_mean: float32 [256], P('gz')
- running_mean: float32 [256], P('gz')
Inputs may be any that keep to these rules, and one draw needn't show every extreme that they name: flow[0], flow[1] and flow[2] lie within -0.1 to 0.1; flow[3] lies within 0.02 to 0.12.
All inputs are finite; a program needn't handle non-finite values.
Results may differ from a plain program's by a relative error of at most 0.00002.
Values sent between devices are 32-bit elements; how exact they have to be, the bound alone decides.
No kernel may reach another device: no remote copies, remote signals or barrier semaphores. Data moves between devices by JAX's collectives and lax.ppermute only.
A program may use at most 128 MiB of HBM per device.

v0:
```python
import functools

import jax
import jax.numpy as jnp
from jax import lax
from jax.experimental import pallas as pl
from jax.experimental.pallas import tpu as pltpu
from jax.sharding import PartitionSpec as P

F32 = jnp.float32
ANY = pl.BlockSpec(memory_space=pl.ANY)
SMEM = pl.BlockSpec(memory_space=pltpu.SMEM)
VMEM = pl.BlockSpec(memory_space=pltpu.VMEM)
HBM = pl.BlockSpec(memory_space=pltpu.HBM)
LANES = 128
ROWS = 8
FIRST = 32
UNROLL = 4


def params(mib=24):
    return pltpu.CompilerParams(vmem_limit_bytes=mib * 2**20)


def rows_of(shape):
    return lax.broadcasted_iota(jnp.int32, shape, 0)


def lanes_of(shape):
    return lax.broadcasted_iota(jnp.int32, shape, 1)


def down(tile, count):
    count %= ROWS
    return pltpu.roll(tile, count, 0) if count else tile


def part_rows(rows, cut):
    rest = rows - cut
    return (5 * cut + ROWS, 2 * rest + ROWS, 3 * rest)


def edge_row(part, rows, cut):
    return 2 * (rows - cut if part else cut)


def segments(field, rows, cut, begin, end):
    rest, found = rows - cut, []
    low, high = max(begin, 0), min(end, cut)
    if low < high:
        at = field * cut if field < 2 else field * cut + ROWS
        found.append((0, at + low, low, high - low))
    low, high = max(begin, cut), min(end, rows)
    if low < high:
        part, at = (1, field * rest) if field < 2 else (2, (field - 2) * rest)
        found.append((part, at + low - cut, low, high - low))
    return found


def pack_body(quarters, rows, cut, slots, parts, idx, energy, flow, *refs):
    count = len(slots) * len(parts)
    outs, (low, high, sem, tile_sem) = refs[:count], refs[count:]
    me = idx[0]
    fields = [energy.at[0]] + [flow.at[c, 0] for c in (3, 0, 1, 2)]
    copies, tiles = [], []
    for n, slot in enumerate(slots):
        first = pl.multiple_of(lax.rem(me + slot, quarters) * rows, ROWS)
        before = pl.multiple_of(jnp.maximum(first - ROWS, 0), ROWS)
        after = pl.multiple_of(jnp.minimum(first + rows, (quarters - 1) * rows), ROWS)
        for f, field in enumerate(fields):
            if 0 in parts:
                tiles.append(
                    pltpu.make_async_copy(field.at[pl.ds(before, ROWS)], low.at[n, f], tile_sem)
                )
            if 1 in parts:
                tiles.append(
                    pltpu.make_async_copy(field.at[pl.ds(after, ROWS)], high.at[n, f], tile_sem)
                )
    for copy in tiles:
        copy.start()
    for n, slot in enumerate(slots):
        first = lax.rem(me + slot, quarters) * rows
        for f, field in enumerate(fields):
            for part, at, row, size in segments(f, rows, cut, 0, rows):
                if part in parts:
                    out = outs[n * len(parts) + parts.index(part)]
                    source = field.at[pl.ds(pl.multiple_of(first + row, ROWS), size)]
                    copies.append(pltpu.make_async_copy(source, out.at[pl.ds(at, size)], sem))
    for copy in copies:
        copy.start()
    for copy in tiles:
        copy.wait()
    shape = low.shape[2:]
    row = rows_of(shape)
    places = ((0, 2), (2, 2), (4, 1), (5, 1), (6, 1))
    for n, slot in enumerate(slots):
        to = lax.rem(me + slot, quarters)
        for part in parts:
            if part == 2:
                continue
            tile = jnp.zeros(shape, F32)
            for f, (begin, size) in enumerate(places):
                here = (row >= begin) & (row < begin + size)
                moved = down(high[n, f], begin) if part else down(low[n, f], begin + size)
                tile = jnp.where(here, moved, tile)
            out = outs[n * len(parts) + parts.index(part)]
            at = edge_row(part, rows, cut)
            out[at : at + ROWS] = jnp.where(to == (quarters - 1 if part else 0), 0.0, tile)
    for copy in copies:
        copy.wait()


def pack(idx, energy, flow, quarters, cut, slots, parts):
    rows, width = energy.shape[1] // quarters, energy.shape[2]
    sizes = part_rows(rows, cut)
    shapes = [jax.ShapeDtypeStruct((sizes[part], width), F32) for part in parts] * len(slots)
    out = pl.pallas_call(
        functools.partial(pack_body, quarters, rows, cut, slots, parts),
        out_shape=shapes,
        in_specs=[SMEM, HBM, HBM],
        out_specs=[VMEM] * len(shapes),
        scratch_shapes=[
            pltpu.VMEM((len(slots), 5, ROWS, width), F32),
            pltpu.VMEM((len(slots), 5, ROWS, width), F32),
            pltpu.SemaphoreType.DMA,
            pltpu.SemaphoreType.DMA,
        ],
        compiler_params=params(),
        name="pack",
    )(idx, energy, flow)
    return [list(out[n * len(parts) : (n + 1) * len(parts)]) for n in range(len(slots))]


def end_planes(idx, quarters):
    above = lax.rem(idx[1], 2) == 0
    return jnp.where(above, quarters - 1, 0), jnp.where(above, 0, quarters - 1)


def beyond(plane):
    return jnp.where(plane == 0, 0, plane + 2)


def ends_body(count, idx, *refs):
    slots, outs = refs[:count], refs[count:]
    for slot, ref in enumerate(slots):
        plane = lax.rem(idx[0] - slot + count, count)
        for wanted, out in zip(end_planes(idx, count), outs):

            @pl.when(plane == wanted)
            def _():
                out[...] = ref[: out.shape[0]]


def ends(idx, slots, rows):
    shape = jax.ShapeDtypeStruct((rows, slots[0].shape[1]), F32)
    return pl.pallas_call(
        functools.partial(ends_body, len(slots)),
        out_shape=[shape] * 2,
        in_specs=[SMEM] + [VMEM] * len(slots),
        out_specs=[VMEM] * 2,
        compiler_params=params(),
        name="ends",
    )(idx, *slots)


def tile_at(ref, plane, row, block):
    return ref[plane, pl.ds(row, ROWS), block * LANES : (block + 1) * LANES]


def neighbours(ref, plane, row, above, below, blocks, block):
    centre = tile_at(ref, plane, row, block)
    r, c = rows_of(centre.shape), lanes_of(centre.shape)
    zero = jnp.zeros_like(centre)
    right = tile_at(ref, plane, row, block + 1) if block + 1 < blocks else zero
    left = tile_at(ref, plane, row, block - 1) if block else zero
    return centre, (
        (tile_at(ref, plane + 1, row, block), tile_at(ref, plane - 1, row, block)),
        (
            pltpu.roll(jnp.where(r == 0, tile_at(ref, plane, above, block), centre), ROWS - 1, 0),
            pltpu.roll(jnp.where(r == ROWS - 1, tile_at(ref, plane, below, block), centre), 1, 0),
        ),
        (
            pltpu.roll(jnp.where(c == 0, right, centre), LANES - 1, 1),
            pltpu.roll(jnp.where(c == LANES - 1, left, centre), 1, 1),
        ),
    )


def stepped(e_ref, k_ref, u_ref, plane, row, blocks, block):
    row = pl.multiple_of(row, ROWS)
    above = pl.multiple_of(jnp.minimum(row + ROWS, e_ref.shape[1] - ROWS), ROWS)
    below = pl.multiple_of(jnp.maximum(row - ROWS, 0), ROWS)
    e, es = neighbours(e_ref, plane + 1, row, above, below, blocks, block)
    k, ks = neighbours(k_ref, plane + 1, row, above, below, blocks, block)
    change = None
    for d in range(3):
        (e_up, e_low), (k_up, k_low) = es[d], ks[d]
        speed = u_ref[d, plane, pl.ds(row, ROWS), block * LANES : (block + 1) * LANES]
        gain = (0.5 * (k + k_up) - jnp.minimum(speed, 0.0)) * (e_up - e)
        loss = (0.5 * (k + k_low) + jnp.maximum(speed, 0.0)) * (e - e_low)
        change = gain - loss if change is None else change + (gain - loss)
    return e + change


def gather_rows(rows, cut, window, span, me, slots, ends, e, k, u):
    begin, end = window
    quarters = len(slots)
    planes = [(lax.rem(me - s + quarters, quarters), parts, True) for s, parts in enumerate(slots)]
    for plane, parts, inside in planes + [(*pair, False) for pair in ends]:
        up = plane + 1 if inside else plane
        for field in range(5 if inside else 2):
            if field == 0 and e is None:
                continue
            for part, at, row, size in segments(
                field, rows, cut, *(window if field < 2 else span)
            ):
                to, value = pl.ds(row - begin, size), parts[part][at : at + size]
                if field < 2:
                    (e, k)[field][up, to] = value
                else:
                    u[field - 2, plane, to] = value
        if begin < 0:
            tile = parts[0][2 * cut : 2 * cut + ROWS]
            if e is not None:
                e[up, :ROWS] = down(tile, 6)
            k[up, :ROWS] = down(tile, 4)
            for d in range(3 if inside and span[0] < 0 else 0):
                u[d, plane, :ROWS] = down(tile, 3 - d)
        if end > rows:
            tile = parts[1][2 * (rows - cut) : 2 * (rows - cut) + ROWS]
            to = pl.ds(end - begin - ROWS, ROWS)
            if e is not None:
                e[up, to] = tile
            k[up, to] = down(tile, -2)
            for d in range(3 if inside and span[1] > rows else 0):
                u[d, plane, to] = down(tile, -4 - d)


def scratch(quarters, tall, width):
    return [
        pltpu.VMEM((quarters + 2, tall, width), F32),
        pltpu.VMEM((quarters + 2, tall, width), F32),
        pltpu.VMEM((3, quarters, tall, width), F32),
    ]


def grouped(refs, counts):
    out = []
    for count in counts:
        out.append(refs[:count])
        refs = refs[count:]
    return out + [refs]


def first_body(rows, cut, window, span, sent, quarters, blocks, given, idx, *refs):
    *slots, even, odd, refs = grouped(refs, [given[0]] * quarters + [given[1]] * 2)
    half, *half_ends, e, k, u = refs
    me = idx[0]
    last = end_planes(idx, quarters)
    ends = [(beyond(plane), parts) for plane, parts in zip(last, (even, odd))]
    gather_rows(rows, cut, window, span, me, slots, ends, e, k, u)
    begin = window[0]
    tiles = (span[1] - span[0]) // ROWS

    def tile_step(n, _):
        plane, at = n // tiles, span[0] + (n % tiles) * ROWS
        outside = ((at < 0) & (me == 0)) | ((at >= rows) & (me == quarters - 1))
        to = pl.ds(pl.multiple_of(at - span[0], ROWS), ROWS)
        for block in range(blocks):
            value = stepped(e, k, u, plane, at - begin, blocks, block)
            value = jnp.where(outside, 0.0, value)
            half[plane, to, block * LANES : (block + 1) * LANES] = value
        return 0

    lax.fori_loop(0, quarters * tiles, tile_step, 0, unroll=UNROLL)
    for plane, ref in zip(last, half_ends):
        ref[...] = half[plane, sent[0] - span[0] : sent[1] - span[0]]


def first_step(idx, slots, even, odd, rows, cut, window, span, sent):
    quarters, width = len(slots), even[0].shape[1]
    given = (len(slots[0]), len(even))
    flat = [x for parts in slots for x in parts] + list(even) + list(odd)
    plane = jax.ShapeDtypeStruct((sent[1] - sent[0], width), F32)
    return pl.pallas_call(
        functools.partial(
            first_body, rows, cut, window, span, sent, quarters, width // LANES, given
        ),
        out_shape=[jax.ShapeDtypeStruct((quarters, span[1] - span[0], width), F32), plane, plane],
        in_specs=[SMEM] + [VMEM] * len(flat),
        out_specs=[VMEM] * 3,
        scratch_shapes=scratch(quarters, window[1] - window[0], width),
        compiler_params=params(),
        name="first_step",
    )(idx, *flat)


def second_body(rows, cut, window, span, quarters, blocks, given, halves, before, idx, *refs):
    *slots, even, odd, half, half_even, half_odd, early, pieces, refs = grouped(
        refs, [given[0]] * quarters + [given[1]] * 2 + [len(halves)] * 3 + [before, blocks // 2]
    )
    total_ref, e, k, u, result, totals = refs
    me, my = idx[0], idx[1]
    outer = [beyond(plane) for plane in end_planes(idx, quarters)]
    ends = list(zip(outer, (even, odd)))
    gather_rows(rows, cut, window, span, me, slots, ends, None, k, u)
    begin = window[0]
    for ref, *sides, (start, row, end) in zip(half, half_even, half_odd, halves):
        if start < end:
            for plane in range(quarters):
                e[plane + 1, row - begin : end - begin] = ref[plane, row - start : end - start]
        first, last = max(row, span[0]), min(end, span[1])
        if first >= last:
            continue
        at = max(start, 0)
        for plane, side in zip(outer, sides):
            e[plane, first - begin : last - begin] = side[first - at : last - at]
    tiles = (span[1] - span[0]) // ROWS
    totals[...] = jnp.zeros(totals.shape, F32)

    def tile_step(n, _):
        plane, at = n // tiles, pl.multiple_of((n % tiles) * ROWS, ROWS)
        values = []
        for block in range(blocks):
            value = stepped(e, k, u, plane, at + (span[0] - begin), blocks, block)
            result[plane, pl.ds(at, ROWS), block * LANES : (block + 1) * LANES] = value
            values.append(value)
        while len(values) > 1:
            values = [a + b for a, b in zip(values[0::2], values[1::2])]
        totals[plane] = totals[plane] + values[0]
        return 0

    lax.fori_loop(0, quarters * tiles, tile_step, 0, unroll=UNROLL)
    lane = lanes_of((ROWS, LANES))
    found = jnp.zeros((ROWS, LANES), F32)
    for plane in range(quarters):
        found = jnp.where(lane == my * quarters + plane, jnp.sum(totals[plane]), found)
    for n in range(blocks):
        lanes = pl.ds(pl.multiple_of(jnp.bitwise_xor(my, n) * LANES, LANES), LANES)
        pieces[n // 2][n % 2] = result[:, :, lanes]
    if before:
        total_ref[...] = jnp.broadcast_to((early[0][...] + found)[:1], total_ref.shape)
    else:
        total_ref[...] = found


def second_step(
    idx, slots, even, odd, half, half_even, half_odd, early, rows, cut, window, span, halves, count
):
    quarters, width = len(slots), half[0].shape[2]
    given, blocks, size = (len(slots[0]), len(even)), width // LANES, span[1] - span[0]
    flat = [x for parts in slots for x in parts] + list(even) + list(odd)
    flat += list(half) + list(half_even) + list(half_odd) + list(early)
    before = len(early)
    shapes = [jax.ShapeDtypeStruct((2, quarters, size, LANES), F32)] * (blocks // 2)
    shapes += [jax.ShapeDtypeStruct((count if before else ROWS, LANES), F32)]
    out = pl.pallas_call(
        functools.partial(
            second_body, rows, cut, window, span, quarters, blocks, given, halves, before
        ),
        out_shape=shapes,
        in_specs=[SMEM] + [VMEM] * len(flat),
        out_specs=[VMEM] * len(shapes),
        scratch_shapes=scratch(quarters, window[1] - window[0], width)
        + [pltpu.VMEM((quarters, size, width), F32), pltpu.VMEM((quarters, ROWS, LANES), F32)],
        compiler_params=params(),
        name="second_step",
    )(idx, *flat)
    return out[:-1], out[-1]


def pass_on_body(counts, *refs):
    *groups, (out,) = grouped(refs, counts)
    row = 0
    for group in groups:
        size = group[0].shape[2]
        for n, pair in enumerate(group):
            out[n, :, row : row + size] = pair[1]
        row += size


def pass_on(groups):
    _, quarters, _, lanes = groups[0][0].shape
    rows = sum(group[0].shape[2] for group in groups)
    flat = [pair for group in groups for pair in group]
    return pl.pallas_call(
        functools.partial(pass_on_body, [len(group) for group in groups]),
        out_shape=jax.ShapeDtypeStruct((len(groups[0]), quarters, rows, lanes), F32),
        in_specs=[VMEM] * len(flat),
        out_specs=VMEM,
        compiler_params=params(),
        name="pass_on",
    )(*flat)


def finish_body(counts, quarters, cells, idx, found, passed, *refs):
    *groups, (out, mean, running, held, sem, held_sem) = grouped(refs, counts)
    my, pieces, row = idx[1], [], 0

    def planes_from(n):
        return pl.ds(jnp.bitwise_xor(my, n) * quarters, quarters)

    for n in range(counts[0]):
        to = out.at[planes_from(2 * n + 1)]
        pieces.append(pltpu.make_async_copy(passed.at[n], to, sem))
    for group in groups:
        size = group[0].shape[2]
        for n, pair in enumerate(group):
            to = out.at[planes_from(2 * n), pl.ds(row, size)]
            pieces.append(pltpu.make_async_copy(pair.at[0], to, sem))
        row += size
    for copy in pieces:
        copy.start()
    planes, stack = held.shape[2], idx[2]

    def stack_sum(stack):
        rows = found[pl.ds(pl.multiple_of(stack * planes, ROWS), planes)]
        tiles = [rows[n : n + ROWS] for n in range(0, planes, ROWS)]
        while len(tiles) > 1:
            tiles = [a + b for a, b in zip(tiles[0::2], tiles[1::2])]
        return tiles[0]

    here = jnp.sum(stack_sum(stack), 0, keepdims=True)
    zero = jnp.zeros((ROWS, LANES), F32)
    lower = lax.fori_loop(0, stack, lambda n, total: total + stack_sum(n), zero)
    lane = lanes_of(here.shape)
    here = here / cells
    until, by = here, 1
    while by < planes:
        until = until + jnp.where(lane >= by, pltpu.roll(until, by, 1), 0.0)
        by *= 2
    until = until + jnp.sum(lower) / cells
    rank = (stack * planes + lane + 1).astype(F32)
    held[0] = here[:, :planes]
    held[1] = (until / rank)[:, :planes]
    lines = [
        pltpu.make_async_copy(held.at[n], line, held_sem) for n, line in enumerate((mean, running))
    ]
    for copy in lines:
        copy.start()
    for copy in pieces + lines:
        copy.wait()


def finish(idx, found, passed, groups, cells):
    pairs, quarters, rows, lanes = passed.shape
    flat = [pair for group in groups for pair in group]
    counts = [len(group) for group in groups]
    planes = 2 * pairs * quarters
    line = jax.ShapeDtypeStruct((1, planes), F32)
    return pl.pallas_call(
        functools.partial(finish_body, counts, quarters, cells),
        out_shape=[jax.ShapeDtypeStruct((planes, rows, lanes), F32), line, line],
        in_specs=[SMEM, VMEM] + [ANY] * (1 + len(flat)),
        out_specs=[ANY] * 3,
        scratch_shapes=[
            pltpu.VMEM((2, 1, planes), F32),
            pltpu.SemaphoreType.DMA,
            pltpu.SemaphoreType.DMA,
        ],
        compiler_params=params(),
        name="finish",
    )(idx, found, passed, *flat)


def shift(size, by):
    return [(i, (i + by) % size) for i in range(size)]


def over_chips(pairs, sides):
    got = [pairs[0]]
    for n, pair in enumerate(pairs[1:], 1):
        where = [(i, i ^ (2 * n)) for i in range(sides)]
        got.append(lax.ppermute(pair, "gy", where))
    return got


def both_steps(energy, flow):
    quarters, sides, stacks = (lax.axis_size(a) for a in ("gx", "gy", "gz"))
    idx = jnp.stack([lax.axis_index(a) for a in ("gx", "gy", "gz")]).astype(jnp.int32)
    rows, cut = energy.shape[1] // quarters, FIRST
    done = cut - ROWS
    cells = energy.shape[1] * energy.shape[2]
    energy = pltpu.with_memory_space_constraint(energy, pltpu.HBM)
    flow = pltpu.with_memory_space_constraint(flow, pltpu.HBM)

    others = (1, *range(quarters - 1, 1, -1))
    sent = pack(idx, energy, flow, quarters, cut, others, (0,))
    later = pack(idx, energy, flow, quarters, cut, others, (1, 2))
    sent = {slot: a + b for slot, a, b in zip(others, sent, later)}
    got = {
        (slot, part): lax.ppermute(sent[slot][part], "gx", shift(quarters, slot))
        for part in range(3)
        for slot in others
    }
    own = pack(idx, energy, flow, quarters, cut, (0,), (0, 1, 2))[0]
    slots = [own] + [[got[slot, part] for part in range(3)] for slot in range(1, quarters)]
    firsts = [parts[:1] for parts in slots]

    def place_of(stack):
        stack %= stacks * sides
        return (stack % sides) * stacks + stack // sides

    def exchanged(even, odd):
        got = []
        for start, value in ((1, odd), (0, even)):
            lows = [(place_of(n), place_of(n + 1)) for n in range(start, stacks * sides, 2)]
            pairs = lows + [(b, a) for a, b in lows]
            got.append(lax.ppermute(value, ("gy", "gz"), pairs))
        return got[1], got[0]

    last = ends(idx, [s[0] for s in slots], 2 * cut + ROWS)
    even, odd = ([x] for x in exchanged(*last))
    args = (rows, cut, (-ROWS, cut), (-ROWS, cut), (0, done))
    half_a, *last = first_step(idx, firsts, even, odd, *args)
    even_a, odd_a = exchanged(*last)
    args = ([half_a], [even_a], [odd_a], (), rows, cut, (-ROWS, cut), (0, done))
    args += (((-ROWS, -ROWS, cut),), 0)
    pieces_a, sums = second_step(idx, firsts, even, odd, *args)
    pieces_a = over_chips(pieces_a, sides)

    last = ends(idx, [s[1] for s in slots], 2 * (rows - cut) + ROWS)
    even, odd = (a + [b] for a, b in zip((even, odd), exchanged(*last)))
    top = rows + ROWS
    args = (rows, cut, (done - ROWS, top), (done, top), (done, rows))
    half_b, *last = first_step(idx, slots, even, odd, *args)
    even_b, odd_b = exchanged(*last)
    args = ([half_a, half_b], [even_a, even_b], [odd_a, odd_b], (sums,), rows, cut)
    args += ((done - ROWS, top), (done, rows), ((-ROWS, done - ROWS, done), (done, done, top)))
    args += (quarters * sides * stacks,)
    pieces_b, sums = second_step(idx, slots, even, odd, *args)
    pieces_b = over_chips(pieces_b, sides)

    everyone = functools.partial(lax.all_to_all, tiled=True)
    found = everyone(sums, ("gz", "gy", "gx"), 0, 0)
    groups = [pieces_a, pieces_b]
    passed = pass_on(groups)
    passed = lax.ppermute(passed, "gy", [(i, i ^ 1) for i in range(sides)])
    out = finish(idx, found, passed, groups, cells)
    return out[0], out[1].reshape(-1), out[2].reshape(-1)


def solution(mesh):
    placed = (P(("gz", "gy", "gx"), None, None), P(None, ("gz", "gy", "gx"), None, None))
    return jax.shard_map(
        both_steps,
        mesh=mesh,
        in_specs=placed,
        out_specs=(P("gz", "gx", "gy"), P("gz"), P("gz")),
        check_vma=False,
    )
```

profile of v0, /device:TPU:1, one launch (start us, length us, event | category | flops | bytes accessed | tf_op | source)
XLA Modules:
  0.0 147.7 jit_solution(778272669965399460)
XLA Ops:
  0.6 0.1 pad_add_fusion.idx
  0.7 2.3 %pack.5 = (f32[72,1024]{1,0:T(8,128)S(1)}, f32[96,1024]{1,0:T(8,128)S(1)}, f32[72,1024]{1,0:T(8,128)S(1)}, f32[96,1024]{1,0:T(8,128)S(1)}, f32[72,1024]{1,0:T(8,128)S(1)}, /*index=5*/f32[96,1024]{1,0:T(8,128)S(1)}) custom-call(s32[3]{0:T(128)S(1)} %pad_add_fusion.idx, f32[1,256,1024]{2,1,0:T(8,128)} %energy.5, f32[4,1,256,1024]{3,2,1,0:T(8,128)} %flow.5), custom_call_target="tpu_custom_call" | custom-call | tf_op jit(solution)/shard_map/pack/pallas_call | solution.py:117
  3.0 2.1 %collective-permute-start.1 = (f32[72,1024]{1,0:T(8,128)S(1)}, f32[72,1024]{1,0:T(8,128)S(1)}, u32[]{:S(2)}, u32[]{:S(2)}) collective-permute-start(f32[72,1024]{1,0:T(8,128)S(1)} %get-tuple-element.42), channel_id=1, source_target_pairs={{0,64},{64,128},{128,192},{192,0},{1,65},{65,129},{129,193},{193,1... | collective-permute-start | bytes 884744 | tf_op jit(solution)/shard_map/ppermute | solution.py:492
  5.1 2.3 %pack.4 = (f32[168,1024]{1,0:T(8,128)S(1)}, f32[168,1024]{1,0:T(8,128)S(1)}, f32[168,1024]{1,0:T(8,128)S(1)}) custom-call(s32[3]{0:T(128)S(1)} %pad_add_fusion.idx, f32[1,256,1024]{2,1,0:T(8,128)} %energy.5, f32[4,1,256,1024]{3,2,1,0:T(8,128)} %flow.5), custom_call_target="tpu_custom_call" | custom-call | tf_op jit(solution)/shard_map/pack/pallas_call | solution.py:117
  7.4 1.3 collective-permute-start
  8.7 1.3 collective-permute-start.3
  10.0 2.0 %collective-permute-start.6 = (f32[168,1024]{1,0:T(8,128)S(1)}, f32[168,1024]{1,0:T(8,128)S(1)}, u32[]{:S(2)}, u32[]{:S(2)}) collective-permute-start(f32[168,1024]{1,0:T(8,128)S(1)} %get-tuple-element.47), channel_id=1, source_target_pairs={{0,192},{64,0},{128,64},{192,128},{1,193},{65,1},{129,65},{193,129... | collective-permute-start | bytes 2064392 | tf_op jit(solution)/shard_map/ppermute | solution.py:492
  12.0 0.5 collective-permute-start.4
  12.5 0.0 collective-permute-done.1.refs_1_.refs_4_
  12.5 1.8 %collective-permute-start.7 = (f32[72,1024]{1,0:T(8,128)S(1)}, f32[72,1024]{1,0:T(8,128)S(1)}, u32[]{:S(2)}, u32[]{:S(2)}) collective-permute-start(f32[72,1024]{1,0:T(8,128)S(1)} %get-tuple-element.48), channel_id=1, source_target_pairs={{0,192},{64,0},{128,64},{192,128},{1,193},{65,1},{129,65},{193,129... | collective-permute-start | bytes 884744 | tf_op jit(solution)/shard_map/ppermute | solution.py:492
  14.3 35.5 %collective-permute-done.4.refs_2_.refs_7_ = f32[72,1024]{1,0:T(8,128)S(1)} collective-permute-done((f32[72,1024]{1,0:T(8,128)S(1)}, f32[72,1024]{1,0:T(8,128)S(1)}, u32[]{:S(2)}, u32[]{:S(2)}) %collective-permute-start.4) | collective-permute-done | bytes 294944 | tf_op jit(solution)/shard_map/ppermute | solution.py:492
  49.8 0.0 collective-permute-start.2
  49.8 3.2 %collective-permute-done.7.refs_3_.refs_10_ = f32[72,1024]{1,0:T(8,128)S(1)} collective-permute-done((f32[72,1024]{1,0:T(8,128)S(1)}, f32[72,1024]{1,0:T(8,128)S(1)}, u32[]{:S(2)}, u32[]{:S(2)}) %collective-permute-start.7) | collective-permute-done | bytes 294944 | tf_op jit(solution)/shard_map/ppermute | solution.py:492
  53.0 2.0 %collective-permute-start.5 = (f32[96,1024]{1,0:T(8,128)S(1)}, f32[96,1024]{1,0:T(8,128)S(1)}, u32[]{:S(2)}, u32[]{:S(2)}) collective-permute-start(f32[96,1024]{1,0:T(8,128)S(1)} %get-tuple-element.46), channel_id=1, source_target_pairs={{0,128},{64,192},{128,0},{192,64},{1,129},{65,193},{129,1},{193,65... | collective-permute-start | bytes 1179656 | tf_op jit(solution)/shard_map/ppermute | solution.py:492
  55.0 0.0 collective-permute-done.refs_1_.refs_3_
  55.0 2.5 %collective-permute-start.8 = (f32[96,1024]{1,0:T(8,128)S(1)}, f32[96,1024]{1,0:T(8,128)S(1)}, u32[]{:S(2)}, u32[]{:S(2)}) collective-permute-start(f32[96,1024]{1,0:T(8,128)S(1)} %get-tuple-element.49), channel_id=1, source_target_pairs={{0,192},{64,0},{128,64},{192,128},{1,193},{65,1},{129,65},{193,129... | collective-permute-start | bytes 1179656 | tf_op jit(solution)/shard_map/ppermute | solution.py:492
  57.5 2.0 %pack.3 = (f32[168,1024]{1,0:T(8,128)S(1)}, f32[72,1024]{1,0:T(8,128)S(1)}, f32[96,1024]{1,0:T(8,128)S(1)}) custom-call(s32[3]{0:T(128)S(1)} %pad_add_fusion.idx, f32[1,256,1024]{2,1,0:T(8,128)} %energy.5, f32[4,1,256,1024]{3,2,1,0:T(8,128)} %flow.5), custom_call_target="tpu_custom_call" | custom-call | tf_op jit(solution)/shard_map/pack/pallas_call | solution.py:117
  59.5 0.6 ends.3
  60.2 0.0 collective-permute-done.3.refs_2_.refs_6_
  60.2 1.5 %collective-permute-start.10 = (f32[72,1024]{1,0:T(8,128)S(1)}, f32[72,1024]{1,0:T(8,128)S(1)}, u32[]{:S(2)}, u32[]{:S(2)}) collective-permute-start(f32[72,1024]{1,0:T(8,128)S(1)} %get-tuple-element.51), channel_id=1, source_target_pairs={{0,8},{16,24},{32,40},{48,56},{1,9},{17,25},{33,41},{49,57},{2,10}... | collective-permute-start | bytes 884744 | tf_op jit(solution)/shard_map/ppermute | solution.py:509
  61.7 0.0 collective-permute-done.6.refs_3_.refs_9_
  61.7 1.6 %collective-permute-start.12 = (f32[72,1024]{1,0:T(8,128)S(1)}, f32[72,1024]{1,0:T(8,128)S(1)}, u32[]{:S(2)}, u32[]{:S(2)}) collective-permute-start(f32[72,1024]{1,0:T(8,128)S(1)} %get-tuple-element.53), channel_id=1, source_target_pairs={{8,16},{24,32},{40,48},{56,1},{9,17},{25,33},{41,49},{57,2},{10,18... | collective-permute-start | bytes 884744 | tf_op jit(solution)/shard_map/ppermute | solution.py:509
  63.3 0.6 ends.2
  64.0 4.6 %collective-permute-done.2.refs_5_ = f32[96,1024]{1,0:T(8,128)S(1)} collective-permute-done((f32[96,1024]{1,0:T(8,128)S(1)}, f32[96,1024]{1,0:T(8,128)S(1)}, u32[]{:S(2)}, u32[]{:S(2)}) %collective-permute-start.2) | collective-permute-done | bytes 393248 | tf_op jit(solution)/shard_map/ppermute | solution.py:492
  68.6 2.4 %collective-permute-start.9 = (f32[72,1024]{1,0:T(8,128)S(1)}, f32[72,1024]{1,0:T(8,128)S(1)}, u32[]{:S(2)}, u32[]{:S(2)}) collective-permute-start(f32[72,1024]{1,0:T(8,128)S(1)} %get-tuple-element.50), channel_id=1, source_target_pairs={{0,8},{16,24},{32,40},{48,56},{1,9},{17,25},{33,41},{49,57},{2,10}... | collective-permute-start | bytes 884744 | tf_op jit(solution)/shard_map/ppermute | solution.py:509
  71.0 0.0 collective-permute-done.5.refs_8_
  71.0 1.5 %collective-permute-start.11 = (f32[72,1024]{1,0:T(8,128)S(1)}, f32[72,1024]{1,0:T(8,128)S(1)}, u32[]{:S(2)}, u32[]{:S(2)}) collective-permute-start(f32[72,1024]{1,0:T(8,128)S(1)} %get-tuple-element.52), channel_id=1, source_target_pairs={{8,16},{24,32},{40,48},{56,1},{9,17},{25,33},{41,49},{57,2},{10,18... | collective-permute-start | bytes 884744 | tf_op jit(solution)/shard_map/ppermute | solution.py:509
  72.5 1.7 %collective-permute-done.8.refs_11_ = f32[96,1024]{1,0:T(8,128)S(1)} collective-permute-done((f32[96,1024]{1,0:T(8,128)S(1)}, f32[96,1024]{1,0:T(8,128)S(1)}, u32[]{:S(2)}, u32[]{:S(2)}) %collective-permute-start.8) | collective-permute-done | bytes 393248 | tf_op jit(solution)/shard_map/ppermute | solution.py:492
  74.2 0.0 collective-permute-done.10.refs_13_
  74.2 0.0 collective-permute-done.12.refs_15_
  74.2 0.0 collective-permute-done.9.refs_4_.refs_12_
  74.2 2.9 %collective-permute-done.11.refs_5_.refs_14_ = f32[72,1024]{1,0:T(8,128)S(1)} collective-permute-done((f32[72,1024]{1,0:T(8,128)S(1)}, f32[72,1024]{1,0:T(8,128)S(1)}, u32[]{:S(2)}, u32[]{:S(2)}) %collective-permute-start.11) | collective-permute-done | bytes 294944 | tf_op jit(solution)/shard_map/ppermute | solution.py:509
  77.1 2.5 %first_step.3 = (f32[4,48,1024]{2,1,0:T(8,128)S(1)}, f32[40,1024]{1,0:T(8,128)S(1)}, f32[40,1024]{1,0:T(8,128)S(1)}) custom-call(s32[3]{0:T(128)S(1)} %pad_add_fusion.idx, f32[168,1024]{1,0:T(8,128)S(1)} %get-tuple-element.38.refs_0_, f32[72,1024]{1,0:T(8,128)S(1)} %get-tuple-element.39.refs_0_.refs_1_, f32[96,1024]{1,0:T(8,128)S(1)} %get-tuple-element.40.refs_2_, ...), custom_call_target="tpu_custom_call" | custom-call | tf_op jit(solution)/shard_map/first_step/pallas_call | solution.py:285
  79.6 6.8 %collective-permute-start.14 = (f32[40,1024]{1,0:T(8,128)S(1)}, f32[40,1024]{1,0:T(8,128)S(1)}, u32[]{:S(2)}, u32[]{:S(2)}) collective-permute-start(f32[40,1024]{1,0:T(8,128)S(1)} %get-tuple-element.57), channel_id=1, source_target_pairs={{0,8},{16,24},{32,40},{48,56},{1,9},{17,25},{33,41},{49,57},{2,10}... | collective-permute-start | bytes 491528 | tf_op jit(solution)/shard_map/ppermute | solution.py:509
  86.4 0.0 collective-permute-start.16
  86.4 2.2 %first_step.2 = (f32[4,40,1024]{2,1,0:T(8,128)S(1)}, f32[24,1024]{1,0:T(8,128)S(1)}, f32[24,1024]{1,0:T(8,128)S(1)}) custom-call(s32[3]{0:T(128)S(1)} %pad_add_fusion.idx, f32[168,1024]{1,0:T(8,128)S(1)} %get-tuple-element.38.refs_0_, f32[168,1024]{1,0:T(8,128)S(1)} %collective-permute-done.refs_1_.refs_3_, ...), custom_call_target="tpu_custom_call" | custom-call | tf_op jit(solution)/shard_map/first_step/pallas_call | solution.py:285
  88.6 5.2 %collective-permute-start.13 = (f32[24,1024]{1,0:T(8,128)S(1)}, f32[24,1024]{1,0:T(8,128)S(1)}, u32[]{:S(2)}, u32[]{:S(2)}) collective-permute-start(f32[24,1024]{1,0:T(8,128)S(1)} %get-tuple-element.56), channel_id=1, source_target_pairs={{0,8},{16,24},{32,40},{48,56},{1,9},{17,25},{33,41},{49,57},{2,10}... | collective-permute-start | bytes 294920 | tf_op jit(solution)/shard_map/ppermute | solution.py:509
  93.8 0.0 collective-permute-start.15
  93.8 0.9 collective-permute-done.13.refs_7_.refs_18_
  94.7 3.1 %collective-permute-done.15.refs_8_.refs_20_ = f32[24,1024]{1,0:T(8,128)S(1)} collective-permute-done((f32[24,1024]{1,0:T(8,128)S(1)}, f32[24,1024]{1,0:T(8,128)S(1)}, u32[]{:S(2)}, u32[]{:S(2)}) %collective-permute-start.15) | collective-permute-done | bytes 98336 | tf_op jit(solution)/shard_map/ppermute | solution.py:509
  97.8 1.7 %second_step.2 = (f32[2,4,24,128]{3,2,1,0:T(8,128)S(1)}, f32[2,4,24,128]{3,2,1,0:T(8,128)S(1)}, f32[2,4,24,128]{3,2,1,0:T(8,128)S(1)}, f32[2,4,24,128]{3,2,1,0:T(8,128)S(1)}, f32[8,128]{1,0:T(8,128)S(1)}) custom-call(s32[3]{0:T(128)S(1)} %pad_add_fusion.idx, f32[168,1024]{1,0:T(8,128)S(1)} %get-tuple-element.38.refs_0_, ...), custom_call_target="tpu_custom_call" | custom-call | tf_op jit(solution)/shard_map/second_step/pallas_call | solution.py:357
  99.5 0.1 collective-permute-start.17
  99.6 0.0 collective-permute-done.14.refs_19_
  99.6 0.0 collective-permute-done.16.refs_21_
  99.7 2.3 %second_step.3 = (f32[2,4,40,128]{3,2,1,0:T(8,128)S(1)}, f32[2,4,40,128]{3,2,1,0:T(8,128)S(1)}, f32[2,4,40,128]{3,2,1,0:T(8,128)S(1)}, f32[2,4,40,128]{3,2,1,0:T(8,128)S(1)}, f32[256,128]{1,0:T(8,128)S(1)}) custom-call(s32[3]{0:T(128)S(1)} %pad_add_fusion.idx, f32[168,1024]{1,0:T(8,128)S(1)} %get-tuple-element.38.refs_0_, ...), custom_call_target="tpu_custom_call" | custom-call | tf_op jit(solution)/shard_map/second_step/pallas_call | solution.py:357
  102.0 1.5 %collective-permute-start.20 = (f32[2,4,40,128]{3,2,1,0:T(8,128)S(1)}, f32[2,4,40,128]{3,2,1,0:T(8,128)S(1)}, u32[]{:S(2)}, u32[]{:S(2)}) collective-permute-start(f32[2,4,40,128]{3,2,1,0:T(8,128)S(1)} %get-tuple-element.67), channel_id=1, source_target_pairs={{0,16},{8,24},{16,0},{24,8},{32,48},{40,56},{48,32},{56,40},{1,17}... | collective-permute-start | bytes 491528 | tf_op jit(solution)/shard_map/ppermute | solution.py:474
  103.5 0.0 collective-permute-start.21
  103.5 2.2 %collective-permute-start.22 = (f32[2,4,40,128]{3,2,1,0:T(8,128)S(1)}, f32[2,4,40,128]{3,2,1,0:T(8,128)S(1)}, u32[]{:S(2)}, u32[]{:S(2)}) collective-permute-start(f32[2,4,40,128]{3,2,1,0:T(8,128)S(1)} %get-tuple-element.69), channel_id=1, source_target_pairs={{0,48},{8,56},{16,32},{24,40},{32,16},{40,24},{48,0},{56,8},{1,49}... | collective-permute-start | bytes 491528 | tf_op jit(solution)/shard_map/ppermute | solution.py:474
  105.7 0.2 collective-permute-start.18
  105.9 0.0 collective-permute-done.17.refs_1_
  105.9 2.4 %collective-permute-start.19 = (f32[2,4,24,128]{3,2,1,0:T(8,128)S(1)}, f32[2,4,24,128]{3,2,1,0:T(8,128)S(1)}, u32[]{:S(2)}, u32[]{:S(2)}) collective-permute-start(f32[2,4,24,128]{3,2,1,0:T(8,128)S(1)} %get-tuple-element.65), channel_id=1, source_target_pairs={{0,48},{8,56},{16,32},{24,40},{32,16},{40,24},{48,0},{56,8},{1,49}... | collective-permute-start | bytes 294920 | tf_op jit(solution)/shard_map/ppermute | solution.py:474
  108.2 19.0 %collective-permute-done.18.refs_2_ = f32[2,4,24,128]{3,2,1,0:T(8,128)S(1)} collective-permute-done((f32[2,4,24,128]{3,2,1,0:T(8,128)S(1)}, f32[2,4,24,128]{3,2,1,0:T(8,128)S(1)}, u32[]{:S(2)}, u32[]{:S(2)}) %collective-permute-start.18) | collective-permute-done | bytes 98336 | tf_op jit(solution)/shard_map/ppermute | solution.py:474
  127.2 0.0 collective-permute-done.19.refs_3_
  127.2 0.0 collective-permute-done.20.refs_5_
  127.2 0.0 collective-permute-done.21.refs_6_
  127.2 0.0 collective-permute-done.22.refs_7_
  127.3 0.7 collective-permute-start.23
  128.0 18.1 %all_to_all.11 = f32[256,1,128]{2,1,0:T(1,128)S(1)} all-to-all(f32[256,1,128]{2,1,0:T(1,128)S(1)} %bitcast.10), channel_id=1, replica_groups=mesh['gx'=4,'gy'=8,'gz'=8] {'gz','gy','gx'}, dimensions={0} | all-to-all | bytes 262144 | tf_op jit(solution)/shard_map/all_to_all | solution.py:535
  146.0 0.0 collective-permute-done.23.passed
  146.0 1.5 %finish.1 = (f32[32,64,128]{2,1,0:T(8,128)}, f32[1,32]{1,0:T(1,128)}, f32[1,32]{1,0:T(1,128)}) custom-call(s32[3]{0:T(128)S(1)} %pad_add_fusion.idx, f32[256,128]{1,0:T(8,128)S(1)} %bitcast.9, f32[4,4,64,128]{3,2,1,0:T(8,128)S(1)} %collective-permute-done.23.passed, f32[2,4,24,128]{3,2,1,0:T(8,128)S(1)} %get-tuple-element.62.refs_0_, ...), custom_call_target="tpu_custom_call" | custom-call | tf_op jit(solution)/shard_map/finish/pallas_call | solution.py:451
  (1 shorter events, 0.0 us)
Async XLA Ops:
  3.0 9.5 %collective-permute-start.1 = (f32[72,1024]{1,0:T(8,128)S(1)}, f32[72,1024]{1,0:T(8,128)S(1)}, u32[]{:S(2)}, u32[]{:S(2)}) collective-permute-start(f32[72,1024]{1,0:T(8,128)S(1)} %get-tuple-element.42), channel_id=1, source_target_pairs={{0,64},{64,128},{128,192},{192,0},{1,65},{65,129},{129,193},{193,1... | collective-permute-start | bytes 884744 | tf_op jit(solution)/shard_map/ppermute | solution.py:492
  7.4 47.6 %collective-permute-start = (f32[168,1024]{1,0:T(8,128)S(1)}, f32[168,1024]{1,0:T(8,128)S(1)}, u32[]{:S(2)}, u32[]{:S(2)}) collective-permute-start(f32[168,1024]{1,0:T(8,128)S(1)} %get-tuple-element.41), channel_id=1, source_target_pairs={{0,64},{64,128},{128,192},{192,0},{1,65},{65,129},{129,193},{193,1... | collective-permute-start | bytes 2064392 | tf_op jit(solution)/shard_map/ppermute | solution.py:492
  8.7 51.5 %collective-permute-start.3 = (f32[168,1024]{1,0:T(8,128)S(1)}, f32[168,1024]{1,0:T(8,128)S(1)}, u32[]{:S(2)}, u32[]{:S(2)}) collective-permute-start(f32[168,1024]{1,0:T(8,128)S(1)} %get-tuple-element.44), channel_id=1, source_target_pairs={{0,128},{64,192},{128,0},{192,64},{1,129},{65,193},{129,1},{193,65... | collective-permute-start | bytes 2064392 | tf_op jit(solution)/shard_map/ppermute | solution.py:492
  10.0 51.7 %collective-permute-start.6 = (f32[168,1024]{1,0:T(8,128)S(1)}, f32[168,1024]{1,0:T(8,128)S(1)}, u32[]{:S(2)}, u32[]{:S(2)}) collective-permute-start(f32[168,1024]{1,0:T(8,128)S(1)} %get-tuple-element.47), channel_id=1, source_target_pairs={{0,192},{64,0},{128,64},{192,128},{1,193},{65,1},{129,65},{193,129... | collective-permute-start | bytes 2064392 | tf_op jit(solution)/shard_map/ppermute | solution.py:492
  12.0 37.8 %collective-permute-start.4 = (f32[72,1024]{1,0:T(8,128)S(1)}, f32[72,1024]{1,0:T(8,128)S(1)}, u32[]{:S(2)}, u32[]{:S(2)}) collective-permute-start(f32[72,1024]{1,0:T(8,128)S(1)} %get-tuple-element.45), channel_id=1, source_target_pairs={{0,128},{64,192},{128,0},{192,64},{1,129},{65,193},{129,1},{193,65... | collective-permute-start | bytes 884744 | tf_op jit(solution)/shard_map/ppermute | solution.py:492
  12.5 40.5 %collective-permute-start.7 = (f32[72,1024]{1,0:T(8,128)S(1)}, f32[72,1024]{1,0:T(8,128)S(1)}, u32[]{:S(2)}, u32[]{:S(2)}) collective-permute-start(f32[72,1024]{1,0:T(8,128)S(1)} %get-tuple-element.48), channel_id=1, source_target_pairs={{0,192},{64,0},{128,64},{192,128},{1,193},{65,1},{129,65},{193,129... | collective-permute-start | bytes 884744 | tf_op jit(solution)/shard_map/ppermute | solution.py:492
  49.8 18.8 %collective-permute-start.2 = (f32[96,1024]{1,0:T(8,128)S(1)}, f32[96,1024]{1,0:T(8,128)S(1)}, u32[]{:S(2)}, u32[]{:S(2)}) collective-permute-start(f32[96,1024]{1,0:T(8,128)S(1)} %get-tuple-element.43), channel_id=1, source_target_pairs={{0,64},{64,128},{128,192},{192,0},{1,65},{65,129},{129,193},{193,1... | collective-permute-start | bytes 1179656 | tf_op jit(solution)/shard_map/ppermute | solution.py:492
  53.0 18.0 %collective-permute-start.5 = (f32[96,1024]{1,0:T(8,128)S(1)}, f32[96,1024]{1,0:T(8,128)S(1)}, u32[]{:S(2)}, u32[]{:S(2)}) collective-permute-start(f32[96,1024]{1,0:T(8,128)S(1)} %get-tuple-element.46), channel_id=1, source_target_pairs={{0,128},{64,192},{128,0},{192,64},{1,129},{65,193},{129,1},{193,65... | collective-permute-start | bytes 1179656 | tf_op jit(solution)/shard_map/ppermute | solution.py:492
  55.0 19.2 %collective-permute-start.8 = (f32[96,1024]{1,0:T(8,128)S(1)}, f32[96,1024]{1,0:T(8,128)S(1)}, u32[]{:S(2)}, u32[]{:S(2)}) collective-permute-start(f32[96,1024]{1,0:T(8,128)S(1)} %get-tuple-element.49), channel_id=1, source_target_pairs={{0,192},{64,0},{128,64},{192,128},{1,193},{65,1},{129,65},{193,129... | collective-permute-start | bytes 1179656 | tf_op jit(solution)/shard_map/ppermute | solution.py:492
  60.2 14.0 %collective-permute-start.10 = (f32[72,1024]{1,0:T(8,128)S(1)}, f32[72,1024]{1,0:T(8,128)S(1)}, u32[]{:S(2)}, u32[]{:S(2)}) collective-permute-start(f32[72,1024]{1,0:T(8,128)S(1)} %get-tuple-element.51), channel_id=1, source_target_pairs={{0,8},{16,24},{32,40},{48,56},{1,9},{17,25},{33,41},{49,57},{2,10}... | collective-permute-start | bytes 884744 | tf_op jit(solution)/shard_map/ppermute | solution.py:509
  61.7 12.5 %collective-permute-start.12 = (f32[72,1024]{1,0:T(8,128)S(1)}, f32[72,1024]{1,0:T(8,128)S(1)}, u32[]{:S(2)}, u32[]{:S(2)}) collective-permute-start(f32[72,1024]{1,0:T(8,128)S(1)} %get-tuple-element.53), channel_id=1, source_target_pairs={{8,16},{24,32},{40,48},{56,1},{9,17},{25,33},{41,49},{57,2},{10,18... | collective-permute-start | bytes 884744 | tf_op jit(solution)/shard_map/ppermute | solution.py:509
  68.6 5.6 %collective-permute-start.9 = (f32[72,1024]{1,0:T(8,128)S(1)}, f32[72,1024]{1,0:T(8,128)S(1)}, u32[]{:S(2)}, u32[]{:S(2)}) collective-permute-start(f32[72,1024]{1,0:T(8,128)S(1)} %get-tuple-element.50), channel_id=1, source_target_pairs={{0,8},{16,24},{32,40},{48,56},{1,9},{17,25},{33,41},{49,57},{2,10}... | collective-permute-start | bytes 884744 | tf_op jit(solution)/shard_map/ppermute | solution.py:509
  71.0 6.1 %collective-permute-start.11 = (f32[72,1024]{1,0:T(8,128)S(1)}, f32[72,1024]{1,0:T(8,128)S(1)}, u32[]{:S(2)}, u32[]{:S(2)}) collective-permute-start(f32[72,1024]{1,0:T(8,128)S(1)} %get-tuple-element.52), channel_id=1, source_target_pairs={{8,16},{24,32},{40,48},{56,1},{9,17},{25,33},{41,49},{57,2},{10,18... | collective-permute-start | bytes 884744 | tf_op jit(solution)/shard_map/ppermute | solution.py:509
  79.6 20.0 %collective-permute-start.14 = (f32[40,1024]{1,0:T(8,128)S(1)}, f32[40,1024]{1,0:T(8,128)S(1)}, u32[]{:S(2)}, u32[]{:S(2)}) collective-permute-start(f32[40,1024]{1,0:T(8,128)S(1)} %get-tuple-element.57), channel_id=1, source_target_pairs={{0,8},{16,24},{32,40},{48,56},{1,9},{17,25},{33,41},{49,57},{2,10}... | collective-permute-start | bytes 491528 | tf_op jit(solution)/shard_map/ppermute | solution.py:509
  86.4 13.2 %collective-permute-start.16 = (f32[40,1024]{1,0:T(8,128)S(1)}, f32[40,1024]{1,0:T(8,128)S(1)}, u32[]{:S(2)}, u32[]{:S(2)}) collective-permute-start(f32[40,1024]{1,0:T(8,128)S(1)} %get-tuple-element.59), channel_id=1, source_target_pairs={{8,16},{24,32},{40,48},{56,1},{9,17},{25,33},{41,49},{57,2},{10,18... | collective-permute-start | bytes 491528 | tf_op jit(solution)/shard_map/ppermute | solution.py:509
  88.6 6.2 %collective-permute-start.13 = (f32[24,1024]{1,0:T(8,128)S(1)}, f32[24,1024]{1,0:T(8,128)S(1)}, u32[]{:S(2)}, u32[]{:S(2)}) collective-permute-start(f32[24,1024]{1,0:T(8,128)S(1)} %get-tuple-element.56), channel_id=1, source_target_pairs={{0,8},{16,24},{32,40},{48,56},{1,9},{17,25},{33,41},{49,57},{2,10}... | collective-permute-start | bytes 294920 | tf_op jit(solution)/shard_map/ppermute | solution.py:509
  93.8 4.0 %collective-permute-start.15 = (f32[24,1024]{1,0:T(8,128)S(1)}, f32[24,1024]{1,0:T(8,128)S(1)}, u32[]{:S(2)}, u32[]{:S(2)}) collective-permute-start(f32[24,1024]{1,0:T(8,128)S(1)} %get-tuple-element.58), channel_id=1, source_target_pairs={{8,16},{24,32},{40,48},{56,1},{9,17},{25,33},{41,49},{57,2},{10,18... | collective-permute-start | bytes 294920 | tf_op jit(solution)/shard_map/ppermute | solution.py:509
  99.5 6.3 %collective-permute-start.17 = (f32[2,4,24,128]{3,2,1,0:T(8,128)S(1)}, f32[2,4,24,128]{3,2,1,0:T(8,128)S(1)}, u32[]{:S(2)}, u32[]{:S(2)}) collective-permute-start(f32[2,4,24,128]{3,2,1,0:T(8,128)S(1)} %get-tuple-element.63), channel_id=1, source_target_pairs={{0,16},{8,24},{16,0},{24,8},{32,48},{40,56},{48,32},{56,40},{1,17}... | collective-permute-start | bytes 294920 | tf_op jit(solution)/shard_map/ppermute | solution.py:474
  102.0 25.2 %collective-permute-start.20 = (f32[2,4,40,128]{3,2,1,0:T(8,128)S(1)}, f32[2,4,40,128]{3,2,1,0:T(8,128)S(1)}, u32[]{:S(2)}, u32[]{:S(2)}) collective-permute-start(f32[2,4,40,128]{3,2,1,0:T(8,128)S(1)} %get-tuple-element.67), channel_id=1, source_target_pairs={{0,16},{8,24},{16,0},{24,8},{32,48},{40,56},{48,32},{56,40},{1,17}... | collective-permute-start | bytes 491528 | tf_op jit(solution)/shard_map/ppermute | solution.py:474
  103.5 23.7 %collective-permute-start.21 = (f32[2,4,40,128]{3,2,1,0:T(8,128)S(1)}, f32[2,4,40,128]{3,2,1,0:T(8,128)S(1)}, u32[]{:S(2)}, u32[]{:S(2)}) collective-permute-start(f32[2,4,40,128]{3,2,1,0:T(8,128)S(1)} %get-tuple-element.68), channel_id=1, source_target_pairs={{0,32},{8,40},{16,48},{24,56},{32,0},{40,8},{48,16},{56,24},{1,33}... | collective-permute-start | bytes 491528 | tf_op jit(solution)/shard_map/ppermute | solution.py:474
  103.5 23.7 %collective-permute-start.22 = (f32[2,4,40,128]{3,2,1,0:T(8,128)S(1)}, f32[2,4,40,128]{3,2,1,0:T(8,128)S(1)}, u32[]{:S(2)}, u32[]{:S(2)}) collective-permute-start(f32[2,4,40,128]{3,2,1,0:T(8,128)S(1)} %get-tuple-element.69), channel_id=1, source_target_pairs={{0,48},{8,56},{16,32},{24,40},{32,16},{40,24},{48,0},{56,8},{1,49}... | collective-permute-start | bytes 491528 | tf_op jit(solution)/shard_map/ppermute | solution.py:474
  105.7 21.5 %collective-permute-start.18 = (f32[2,4,24,128]{3,2,1,0:T(8,128)S(1)}, f32[2,4,24,128]{3,2,1,0:T(8,128)S(1)}, u32[]{:S(2)}, u32[]{:S(2)}) collective-permute-start(f32[2,4,24,128]{3,2,1,0:T(8,128)S(1)} %get-tuple-element.64), channel_id=1, source_target_pairs={{0,32},{8,40},{16,48},{24,56},{32,0},{40,8},{48,16},{56,24},{1,33}... | collective-permute-start | bytes 294920 | tf_op jit(solution)/shard_map/ppermute | solution.py:474
  105.9 21.3 %collective-permute-start.19 = (f32[2,4,24,128]{3,2,1,0:T(8,128)S(1)}, f32[2,4,24,128]{3,2,1,0:T(8,128)S(1)}, u32[]{:S(2)}, u32[]{:S(2)}) collective-permute-start(f32[2,4,24,128]{3,2,1,0:T(8,128)S(1)} %get-tuple-element.65), channel_id=1, source_target_pairs={{0,48},{8,56},{16,32},{24,40},{32,16},{40,24},{48,0},{56,8},{1,49}... | collective-permute-start | bytes 294920 | tf_op jit(solution)/shard_map/ppermute | solution.py:474
  127.3 18.7 %collective-permute-start.23 = (f32[4,4,64,128]{3,2,1,0:T(8,128)S(1)}, f32[4,4,64,128]{3,2,1,0:T(8,128)S(1)}, u32[]{:S(2)}, u32[]{:S(2)}) collective-permute-start(f32[4,4,64,128]{3,2,1,0:T(8,128)S(1)} %pass_on.1), channel_id=1, source_target_pairs={{0,8},{8,0},{16,24},{24,16},{32,40},{40,32},{48,56},{56,48},{1,9},... | collective-permute-start | bytes 1572872 | tf_op jit(solution)/shard_map/ppermute | solution.py:538
where the time goes:
time: 148 us
  waiting for transfers between devices  71 us (48%)
  starting transfers between devices  39.6 us (27%)
  Pallas kernels  18.1 us (12%)
  blocking collectives  18.1 us (12%)
    ppermute x9, waiting for transfers between devices, both_steps(): lax.ppermute(sent[slot][part], 'gx', shift(quarters, slot))  45 us
    ppermute x8, starting transfers between devices, exchanged(): got.append(lax.ppermute(value, ('gy', 'gz'), pairs))  19.1 us
    ppermute x6, waiting for transfers between devices, over_chips(): got.append(lax.ppermute(pair, 'gy', where))  19 us
    all_to_all x1, blocking collectives, both_steps(): found = everyone(sums, ('gz', 'gy', 'gx'), 0, 0)  18.1 us
    ppermute x9, starting transfers between devices, both_steps(): lax.ppermute(sent[slot][part], 'gx', shift(quarters, slot))  13.5 us
    ppermute x8, waiting for transfers between devices, exchanged(): got.append(lax.ppermute(value, ('gy', 'gz'), pairs))  7 us
    pallas_call x3, Pallas kernels, pack(): pl.pallas_call(functools.partial(pack_body, quarters, rows, cut, slots, p...  6.58 us
    ppermute x6, starting transfers between devices, over_chips(): got.append(lax.ppermute(pair, 'gy', where))  6.33 us
  transfers between devices with their start and end apart: 24, of which 8 were waited for; matrix products, arithmetic and copies ran while one was open for 0% of the time, Pallas kernels for 8%

commit v1 on v0

--- a/solution.py
+++ b/solution.py
@@ -252,9 +252,11 @@
     return out + [refs]
 
 
-def first_body(rows, cut, window, span, sent, quarters, blocks, given, idx, *refs):
+def first_body(rows, cut, window, span, sent, chosen, quarters, blocks, given, idx, *refs):
     *slots, even, odd, refs = grouped(refs, [given[0]] * quarters + [given[1]] * 2)
-    half, *half_ends, e, k, u = refs
+    half, *half_ends = refs[:-3]
+    e, k, u = refs[-3:]
+    lowest, stride, count = chosen
     me = idx[0]
     last = end_planes(idx, quarters)
     ends = [(beyond(plane), parts) for plane, parts in zip(last, (even, odd))]
@@ -263,32 +265,34 @@
     tiles = (span[1] - span[0]) // ROWS
 
     def tile_step(n, _):
-        plane, at = n // tiles, span[0] + (n % tiles) * ROWS
+        place, at = n // tiles, span[0] + (n % tiles) * ROWS
+        plane = lowest + place * stride
         outside = ((at < 0) & (me == 0)) | ((at >= rows) & (me == quarters - 1))
         to = pl.ds(pl.multiple_of(at - span[0], ROWS), ROWS)
         for block in range(blocks):
             value = stepped(e, k, u, plane, at - begin, blocks, block)
             value = jnp.where(outside, 0.0, value)
-            half[plane, to, block * LANES : (block + 1) * LANES] = value
+            half[place, to, block * LANES : (block + 1) * LANES] = value
         return 0
 
-    lax.fori_loop(0, quarters * tiles, tile_step, 0, unroll=UNROLL)
+    lax.fori_loop(0, count * tiles, tile_step, 0, unroll=UNROLL)
     for plane, ref in zip(last, half_ends):
-        ref[...] = half[plane, sent[0] - span[0] : sent[1] - span[0]]
-
-
-def first_step(idx, slots, even, odd, rows, cut, window, span, sent):
+        place = jnp.where(plane == 0, 0, count - 1)
+        ref[...] = half[place, sent[0] - span[0] : sent[1] - span[0]]
+
+
+def first_step(idx, slots, even, odd, rows, cut, window, span, sent, chosen):
     quarters, width = len(slots), even[0].shape[1]
     given = (len(slots[0]), len(even))
     flat = [x for parts in slots for x in parts] + list(even) + list(odd)
-    plane = jax.ShapeDtypeStruct((sent[1] - sent[0], width), F32)
+    ends = [jax.ShapeDtypeStruct((sent[1] - sent[0], width), F32)] * (2 if sent[0] < sent[1] else 0)
     return pl.pallas_call(
         functools.partial(
-            first_body, rows, cut, window, span, sent, quarters, width // LANES, given
+            first_body, rows, cut, window, span, sent, chosen, quarters, width // LANES, given
         ),
-        out_shape=[jax.ShapeDtypeStruct((quarters, span[1] - span[0], width), F32), plane, plane],
+        out_shape=[jax.ShapeDtypeStruct((chosen[2], span[1] - span[0], width), F32), *ends],
         in_specs=[SMEM] + [VMEM] * len(flat),
-        out_specs=[VMEM] * 3,
+        out_specs=[VMEM] * (1 + len(ends)),
         scratch_shapes=scratch(quarters, window[1] - window[0], width),
         compiler_params=params(),
         name="first_step",
@@ -305,12 +309,12 @@
     ends = list(zip(outer, (even, odd)))
     gather_rows(rows, cut, window, span, me, slots, ends, None, k, u)
     begin = window[0]
-    for ref, *sides, (start, row, end) in zip(half, half_even, half_odd, halves):
+    for ref, *sides, (start, row, end, own, given) in zip(half, half_even, half_odd, halves):
         if start < end:
-            for plane in range(quarters):
-                e[plane + 1, row - begin : end - begin] = ref[plane, row - start : end - start]
+            for place, plane in enumerate(own):
+                e[plane + 1, row - begin : end - begin] = ref[place, row - start : end - start]
         first, last = max(row, span[0]), min(end, span[1])
-        if first >= last:
+        if first >= last or not given:
             continue
         at = max(start, 0)
         for plane, side in zip(outer, sides):
@@ -511,22 +515,32 @@
 
     last = ends(idx, [s[0] for s in slots], 2 * cut + ROWS)
     even, odd = ([x] for x in exchanged(*last))
-    args = (rows, cut, (-ROWS, cut), (-ROWS, cut), (0, done))
+    every = tuple(range(quarters))
+    args = (rows, cut, (-ROWS, cut), (-ROWS, cut), (0, done), (0, 1, quarters))
     half_a, *last = first_step(idx, firsts, even, odd, *args)
     even_a, odd_a = exchanged(*last)
     args = ([half_a], [even_a], [odd_a], (), rows, cut, (-ROWS, cut), (0, done))
-    args += (((-ROWS, -ROWS, cut),), 0)
+    args += (((-ROWS, -ROWS, cut, every, True),), 0)
     pieces_a, sums = second_step(idx, firsts, even, odd, *args)
     pieces_a = over_chips(pieces_a, sides)
 
     last = ends(idx, [s[1] for s in slots], 2 * (rows - cut) + ROWS)
     even, odd = (a + [b] for a, b in zip((even, odd), exchanged(*last)))
     top = rows + ROWS
-    args = (rows, cut, (done - ROWS, top), (done, top), (done, rows))
-    half_b, *last = first_step(idx, slots, even, odd, *args)
+    args = (rows, cut, (done - ROWS, top), (done, top))
+    outer, inner = (0, quarters - 1, 2), (1, 1, quarters - 2)
+    half_b, *last = first_step(idx, slots, even, odd, *args, (done, rows), outer)
     even_b, odd_b = exchanged(*last)
-    args = ([half_a, half_b], [even_a, even_b], [odd_a, odd_b], (sums,), rows, cut)
-    args += ((done - ROWS, top), (done, rows), ((-ROWS, done - ROWS, done), (done, done, top)))
+    (half_c,) = first_step(idx, slots, even, odd, *args, (0, 0), inner)
+    halves = [half_a, half_b, half_c], [even_a, even_b, even_b], [odd_a, odd_b, odd_b]
+    args = (*halves, (sums,), rows, cut, (done - ROWS, top), (done, rows))
+    args += (
+        (
+            (-ROWS, done - ROWS, done, every, False),
+            (done, done, top, (0, quarters - 1), True),
+            (done, done, top, every[1:-1], False),
+        ),
+    )
     args += (quarters * sides * stacks,)
     pieces_b, sums = second_step(idx, slots, even, odd, *args)
     pieces_b = over_chips(pieces_b, sides)

time: 148 us -> 149 us (level)
    pallas_call x2 -> x3, Pallas kernels: 4.66 us -> 5.55 us  [first_step(): pl.pallas_call(functools.partial(first_body, rows, cut, window, span, sen...]
  transfers between devices with their start and end apart: 24 -> 24, of which waited for: 8 -> 8; matrix products, arithmetic and copies ran while one was open for 0% -> 0% of each run, Pallas kernels for 8% -> 9%
where the time goes in v1:
time: 149 us
  waiting for transfers between devices  71 us (48%)
  starting transfers between devices  39.6 us (27%)
  Pallas kernels  19 us (13%)
  blocking collectives  18 us (12%)
    ppermute x9, waiting for transfers between devices, both_steps(): lax.ppermute(sent[slot][part], 'gx', shift(quarters, slot))  45 us
    ppermute x8, starting transfers between devices, exchanged(): got.append(lax.ppermute(value, ('gy', 'gz'), pairs))  19.1 us
    ppermute x6, waiting for transfers between devices, over_chips(): got.append(lax.ppermute(pair, 'gy', where))  19 us
    all_to_all x1, blocking collectives, both_steps(): found = everyone(sums, ('gz', 'gy', 'gx'), 0, 0)  18 us
    ppermute x9, starting transfers between devices, both_steps(): lax.ppermute(sent[slot][part], 'gx', shift(quarters, slot))  13.5 us
    ppermute x8, waiting for transfers between devices, exchanged(): got.append(lax.ppermute(value, ('gy', 'gz'), pairs))  7 us
    pallas_call x3, Pallas kernels, pack(): pl.pallas_call(functools.partial(pack_body, quarters, rows, cut, slots, p...  6.58 us
    ppermute x6, starting transfers between devices, over_chips(): got.append(lax.ppermute(pair, 'gy', where))  6.35 us
  transfers between devices with their start and end apart: 24, of which 8 were waited for; matrix products, arithmetic and copies ran while one was open for 0% of the time, Pallas kernels for 9%

profile of v1, /device:TPU:1, one launch (start us, length us, event | category | flops | bytes accessed | tf_op | source)
XLA Modules:
  0.0 148.6 jit_solution(5371752560736771153)
XLA Ops:
  0.6 0.1 pad_add_fusion.idx
  0.7 2.3 %pack.5 = (f32[72,1024]{1,0:T(8,128)S(1)}, f32[96,1024]{1,0:T(8,128)S(1)}, f32[72,1024]{1,0:T(8,128)S(1)}, f32[96,1024]{1,0:T(8,128)S(1)}, f32[72,1024]{1,0:T(8,128)S(1)}, /*index=5*/f32[96,1024]{1,0:T(8,128)S(1)}) custom-call(s32[3]{0:T(128)S(1)} %pad_add_fusion.idx, f32[1,256,1024]{2,1,0:T(8,128)} %energy.5, f32[4,1,256,1024]{3,2,1,0:T(8,128)} %flow.5), custom_call_target="tpu_custom_call" | custom-call | tf_op jit(solution)/shard_map/pack/pallas_call | solution.py:117
  3.0 2.1 %collective-permute-start.1 = (f32[72,1024]{1,0:T(8,128)S(1)}, f32[72,1024]{1,0:T(8,128)S(1)}, u32[]{:S(2)}, u32[]{:S(2)}) collective-permute-start(f32[72,1024]{1,0:T(8,128)S(1)} %get-tuple-element.42), channel_id=1, source_target_pairs={{0,64},{64,128},{128,192},{192,0},{1,65},{65,129},{129,193},{193,1... | collective-permute-start | bytes 884744 | tf_op jit(solution)/shard_map/ppermute | solution.py:496
  5.1 2.3 %pack.4 = (f32[168,1024]{1,0:T(8,128)S(1)}, f32[168,1024]{1,0:T(8,128)S(1)}, f32[168,1024]{1,0:T(8,128)S(1)}) custom-call(s32[3]{0:T(128)S(1)} %pad_add_fusion.idx, f32[1,256,1024]{2,1,0:T(8,128)} %energy.5, f32[4,1,256,1024]{3,2,1,0:T(8,128)} %flow.5), custom_call_target="tpu_custom_call" | custom-call | tf_op jit(solution)/shard_map/pack/pallas_call | solution.py:117
  7.4 1.3 collective-permute-start
  8.7 1.3 collective-permute-start.3
  10.0 2.0 %collective-permute-start.6 = (f32[168,1024]{1,0:T(8,128)S(1)}, f32[168,1024]{1,0:T(8,128)S(1)}, u32[]{:S(2)}, u32[]{:S(2)}) collective-permute-start(f32[168,1024]{1,0:T(8,128)S(1)} %get-tuple-element.47), channel_id=1, source_target_pairs={{0,192},{64,0},{128,64},{192,128},{1,193},{65,1},{129,65},{193,129... | collective-permute-start | bytes 2064392 | tf_op jit(solution)/shard_map/ppermute | solution.py:496
  12.0 0.5 collective-permute-start.4
  12.5 0.0 collective-permute-done.1.refs_1_.refs_4_
  12.5 1.8 %collective-permute-start.7 = (f32[72,1024]{1,0:T(8,128)S(1)}, f32[72,1024]{1,0:T(8,128)S(1)}, u32[]{:S(2)}, u32[]{:S(2)}) collective-permute-start(f32[72,1024]{1,0:T(8,128)S(1)} %get-tuple-element.48), channel_id=1, source_target_pairs={{0,192},{64,0},{128,64},{192,128},{1,193},{65,1},{129,65},{193,129... | collective-permute-start | bytes 884744 | tf_op jit(solution)/shard_map/ppermute | solution.py:496
  14.3 35.5 %collective-permute-done.4.refs_2_.refs_7_ = f32[72,1024]{1,0:T(8,128)S(1)} collective-permute-done((f32[72,1024]{1,0:T(8,128)S(1)}, f32[72,1024]{1,0:T(8,128)S(1)}, u32[]{:S(2)}, u32[]{:S(2)}) %collective-permute-start.4) | collective-permute-done | bytes 294944 | tf_op jit(solution)/shard_map/ppermute | solution.py:496
  49.8 0.0 collective-permute-start.2
  49.8 3.2 %collective-permute-done.7.refs_3_.refs_10_ = f32[72,1024]{1,0:T(8,128)S(1)} collective-permute-done((f32[72,1024]{1,0:T(8,128)S(1)}, f32[72,1024]{1,0:T(8,128)S(1)}, u32[]{:S(2)}, u32[]{:S(2)}) %collective-permute-start.7) | collective-permute-done | bytes 294944 | tf_op jit(solution)/shard_map/ppermute | solution.py:496
  53.0 2.0 %collective-permute-start.5 = (f32[96,1024]{1,0:T(8,128)S(1)}, f32[96,1024]{1,0:T(8,128)S(1)}, u32[]{:S(2)}, u32[]{:S(2)}) collective-permute-start(f32[96,1024]{1,0:T(8,128)S(1)} %get-tuple-element.46), channel_id=1, source_target_pairs={{0,128},{64,192},{128,0},{192,64},{1,129},{65,193},{129,1},{193,65... | collective-permute-start | bytes 1179656 | tf_op jit(solution)/shard_map/ppermute | solution.py:496
  55.0 0.0 collective-permute-done.refs_1_.refs_3_
  55.0 2.5 %collective-permute-start.8 = (f32[96,1024]{1,0:T(8,128)S(1)}, f32[96,1024]{1,0:T(8,128)S(1)}, u32[]{:S(2)}, u32[]{:S(2)}) collective-permute-start(f32[96,1024]{1,0:T(8,128)S(1)} %get-tuple-element.49), channel_id=1, source_target_pairs={{0,192},{64,0},{128,64},{192,128},{1,193},{65,1},{129,65},{193,129... | collective-permute-start | bytes 1179656 | tf_op jit(solution)/shard_map/ppermute | solution.py:496
  57.5 2.0 %pack.3 = (f32[168,1024]{1,0:T(8,128)S(1)}, f32[72,1024]{1,0:T(8,128)S(1)}, f32[96,1024]{1,0:T(8,128)S(1)}) custom-call(s32[3]{0:T(128)S(1)} %pad_add_fusion.idx, f32[1,256,1024]{2,1,0:T(8,128)} %energy.5, f32[4,1,256,1024]{3,2,1,0:T(8,128)} %flow.5), custom_call_target="tpu_custom_call" | custom-call | tf_op jit(solution)/shard_map/pack/pallas_call | solution.py:117
  59.5 0.6 ends.3
  60.2 0.0 collective-permute-done.3.refs_2_.refs_6_
  60.2 1.5 %collective-permute-start.10 = (f32[72,1024]{1,0:T(8,128)S(1)}, f32[72,1024]{1,0:T(8,128)S(1)}, u32[]{:S(2)}, u32[]{:S(2)}) collective-permute-start(f32[72,1024]{1,0:T(8,128)S(1)} %get-tuple-element.51), channel_id=1, source_target_pairs={{0,8},{16,24},{32,40},{48,56},{1,9},{17,25},{33,41},{49,57},{2,10}... | collective-permute-start | bytes 884744 | tf_op jit(solution)/shard_map/ppermute | solution.py:513
  61.7 0.0 collective-permute-done.6.refs_3_.refs_9_
  61.7 1.6 %collective-permute-start.12 = (f32[72,1024]{1,0:T(8,128)S(1)}, f32[72,1024]{1,0:T(8,128)S(1)}, u32[]{:S(2)}, u32[]{:S(2)}) collective-permute-start(f32[72,1024]{1,0:T(8,128)S(1)} %get-tuple-element.53), channel_id=1, source_target_pairs={{8,16},{24,32},{40,48},{56,1},{9,17},{25,33},{41,49},{57,2},{10,18... | collective-permute-start | bytes 884744 | tf_op jit(solution)/shard_map/ppermute | solution.py:513
  63.3 0.6 ends.2
  64.0 4.6 %collective-permute-done.2.refs_5_ = f32[96,1024]{1,0:T(8,128)S(1)} collective-permute-done((f32[96,1024]{1,0:T(8,128)S(1)}, f32[96,1024]{1,0:T(8,128)S(1)}, u32[]{:S(2)}, u32[]{:S(2)}) %collective-permute-start.2) | collective-permute-done | bytes 393248 | tf_op jit(solution)/shard_map/ppermute | solution.py:496
  68.6 2.4 %collective-permute-start.9 = (f32[72,1024]{1,0:T(8,128)S(1)}, f32[72,1024]{1,0:T(8,128)S(1)}, u32[]{:S(2)}, u32[]{:S(2)}) collective-permute-start(f32[72,1024]{1,0:T(8,128)S(1)} %get-tuple-element.50), channel_id=1, source_target_pairs={{0,8},{16,24},{32,40},{48,56},{1,9},{17,25},{33,41},{49,57},{2,10}... | collective-permute-start | bytes 884744 | tf_op jit(solution)/shard_map/ppermute | solution.py:513
  71.0 0.0 collective-permute-done.5.refs_8_
  71.0 1.5 %collective-permute-start.11 = (f32[72,1024]{1,0:T(8,128)S(1)}, f32[72,1024]{1,0:T(8,128)S(1)}, u32[]{:S(2)}, u32[]{:S(2)}) collective-permute-start(f32[72,1024]{1,0:T(8,128)S(1)} %get-tuple-element.52), channel_id=1, source_target_pairs={{8,16},{24,32},{40,48},{56,1},{9,17},{25,33},{41,49},{57,2},{10,18... | collective-permute-start | bytes 884744 | tf_op jit(solution)/shard_map/ppermute | solution.py:513
  72.5 1.7 %collective-permute-done.8.refs_11_ = f32[96,1024]{1,0:T(8,128)S(1)} collective-permute-done((f32[96,1024]{1,0:T(8,128)S(1)}, f32[96,1024]{1,0:T(8,128)S(1)}, u32[]{:S(2)}, u32[]{:S(2)}) %collective-permute-start.8) | collective-permute-done | bytes 393248 | tf_op jit(solution)/shard_map/ppermute | solution.py:496
  74.2 0.0 collective-permute-done.10.refs_13_
  74.2 0.0 collective-permute-done.12.refs_15_
  74.2 0.0 collective-permute-done.9.refs_4_.refs_12_
  74.2 2.9 %collective-permute-done.11.refs_5_.refs_14_ = f32[72,1024]{1,0:T(8,128)S(1)} collective-permute-done((f32[72,1024]{1,0:T(8,128)S(1)}, f32[72,1024]{1,0:T(8,128)S(1)}, u32[]{:S(2)}, u32[]{:S(2)}) %collective-permute-start.11) | collective-permute-done | bytes 294944 | tf_op jit(solution)/shard_map/ppermute | solution.py:513
  77.1 1.7 %first_step.4 = (f32[2,48,1024]{2,1,0:T(8,128)S(1)}, f32[40,1024]{1,0:T(8,128)S(1)}, f32[40,1024]{1,0:T(8,128)S(1)}) custom-call(s32[3]{0:T(128)S(1)} %pad_add_fusion.idx, f32[168,1024]{1,0:T(8,128)S(1)} %get-tuple-element.38.refs_0_, f32[72,1024]{1,0:T(8,128)S(1)} %get-tuple-element.39.refs_0_.refs_1_, f32[96,1024]{1,0:T(8,128)S(1)} %get-tuple-element.40.refs_2_, ...), custom_call_target="tpu_custom_call" | custom-call | tf_op jit(solution)/shard_map/first_step/pallas_call | solution.py:289
  78.8 6.8 %collective-permute-start.14 = (f32[40,1024]{1,0:T(8,128)S(1)}, f32[40,1024]{1,0:T(8,128)S(1)}, u32[]{:S(2)}, u32[]{:S(2)}) collective-permute-start(f32[40,1024]{1,0:T(8,128)S(1)} %get-tuple-element.57), channel_id=1, source_target_pairs={{0,8},{16,24},{32,40},{48,56},{1,9},{17,25},{33,41},{49,57},{2,10}... | collective-permute-start | bytes 491528 | tf_op jit(solution)/shard_map/ppermute | solution.py:513
  85.6 0.0 collective-permute-start.16
  85.6 2.2 %first_step.3 = (f32[4,40,1024]{2,1,0:T(8,128)S(1)}, f32[24,1024]{1,0:T(8,128)S(1)}, f32[24,1024]{1,0:T(8,128)S(1)}) custom-call(s32[3]{0:T(128)S(1)} %pad_add_fusion.idx, f32[168,1024]{1,0:T(8,128)S(1)} %get-tuple-element.38.refs_0_, f32[168,1024]{1,0:T(8,128)S(1)} %collective-permute-done.refs_1_.refs_3_, ...), custom_call_target="tpu_custom_call" | custom-call | tf_op jit(solution)/shard_map/first_step/pallas_call | solution.py:289
  87.8 5.2 %collective-permute-start.13 = (f32[24,1024]{1,0:T(8,128)S(1)}, f32[24,1024]{1,0:T(8,128)S(1)}, u32[]{:S(2)}, u32[]{:S(2)}) collective-permute-start(f32[24,1024]{1,0:T(8,128)S(1)} %get-tuple-element.56), channel_id=1, source_target_pairs={{0,8},{16,24},{32,40},{48,56},{1,9},{17,25},{33,41},{49,57},{2,10}... | collective-permute-start | bytes 294920 | tf_op jit(solution)/shard_map/ppermute | solution.py:513
  93.0 0.0 collective-permute-start.15
  93.0 0.9 collective-permute-done.13.refs_7_.refs_19_
  93.9 3.1 %collective-permute-done.15.refs_8_.refs_22_ = f32[24,1024]{1,0:T(8,128)S(1)} collective-permute-done((f32[24,1024]{1,0:T(8,128)S(1)}, f32[24,1024]{1,0:T(8,128)S(1)}, u32[]{:S(2)}, u32[]{:S(2)}) %collective-permute-start.15) | collective-permute-done | bytes 98336 | tf_op jit(solution)/shard_map/ppermute | solution.py:513
  97.0 1.7 %second_step.2 = (f32[2,4,24,128]{3,2,1,0:T(8,128)S(1)}, f32[2,4,24,128]{3,2,1,0:T(8,128)S(1)}, f32[2,4,24,128]{3,2,1,0:T(8,128)S(1)}, f32[2,4,24,128]{3,2,1,0:T(8,128)S(1)}, f32[8,128]{1,0:T(8,128)S(1)}) custom-call(s32[3]{0:T(128)S(1)} %pad_add_fusion.idx, f32[168,1024]{1,0:T(8,128)S(1)} %get-tuple-element.38.refs_0_, ...), custom_call_target="tpu_custom_call" | custom-call | tf_op jit(solution)/shard_map/second_step/pallas_call | solution.py:361
  98.7 0.1 collective-permute-start.17
  98.8 1.7 %first_step.5.refs_18_ = f32[2,48,1024]{2,1,0:T(8,128)S(1)} custom-call(s32[3]{0:T(128)S(1)} %pad_add_fusion.idx, f32[168,1024]{1,0:T(8,128)S(1)} %get-tuple-element.38.refs_0_, f32[72,1024]{1,0:T(8,128)S(1)} %get-tuple-element.39.refs_0_.refs_1_, f32[96,1024]{1,0:T(8,128)S(1)} %get-tuple-element.40.refs_2_, ...), custom_call_target="tpu_custom_call" | custom-call | tf_op jit(solution)/shard_map/first_step/pallas_call | solution.py:289
  100.5 0.0 collective-permute-done.14.refs_20_.refs_21_
  100.5 0.0 collective-permute-done.16.refs_23_.refs_24_
  100.5 2.4 %second_step.3 = (f32[2,4,40,128]{3,2,1,0:T(8,128)S(1)}, f32[2,4,40,128]{3,2,1,0:T(8,128)S(1)}, f32[2,4,40,128]{3,2,1,0:T(8,128)S(1)}, f32[2,4,40,128]{3,2,1,0:T(8,128)S(1)}, f32[256,128]{1,0:T(8,128)S(1)}) custom-call(s32[3]{0:T(128)S(1)} %pad_add_fusion.idx, f32[168,1024]{1,0:T(8,128)S(1)} %get-tuple-element.38.refs_0_, ...), custom_call_target="tpu_custom_call" | custom-call | tf_op jit(solution)/shard_map/second_step/pallas_call | solution.py:361
  102.9 1.5 %collective-permute-start.20 = (f32[2,4,40,128]{3,2,1,0:T(8,128)S(1)}, f32[2,4,40,128]{3,2,1,0:T(8,128)S(1)}, u32[]{:S(2)}, u32[]{:S(2)}) collective-permute-start(f32[2,4,40,128]{3,2,1,0:T(8,128)S(1)} %get-tuple-element.67), channel_id=1, source_target_pairs={{0,16},{8,24},{16,0},{24,8},{32,48},{40,56},{48,32},{56,40},{1,17}... | collective-permute-start | bytes 491528 | tf_op jit(solution)/shard_map/ppermute | solution.py:478
  104.4 0.0 collective-permute-start.21
  104.4 2.2 %collective-permute-start.22 = (f32[2,4,40,128]{3,2,1,0:T(8,128)S(1)}, f32[2,4,40,128]{3,2,1,0:T(8,128)S(1)}, u32[]{:S(2)}, u32[]{:S(2)}) collective-permute-start(f32[2,4,40,128]{3,2,1,0:T(8,128)S(1)} %get-tuple-element.69), channel_id=1, source_target_pairs={{0,48},{8,56},{16,32},{24,40},{32,16},{40,24},{48,0},{56,8},{1,49}... | collective-permute-start | bytes 491528 | tf_op jit(solution)/shard_map/ppermute | solution.py:478
  106.6 0.2 collective-permute-start.18
  106.8 0.0 collective-permute-done.17.refs_1_
  106.8 2.4 %collective-permute-start.19 = (f32[2,4,24,128]{3,2,1,0:T(8,128)S(1)}, f32[2,4,24,128]{3,2,1,0:T(8,128)S(1)}, u32[]{:S(2)}, u32[]{:S(2)}) collective-permute-start(f32[2,4,24,128]{3,2,1,0:T(8,128)S(1)} %get-tuple-element.65), channel_id=1, source_target_pairs={{0,48},{8,56},{16,32},{24,40},{32,16},{40,24},{48,0},{56,8},{1,49}... | collective-permute-start | bytes 294920 | tf_op jit(solution)/shard_map/ppermute | solution.py:478
  109.2 19.0 %collective-permute-done.18.refs_2_ = f32[2,4,24,128]{3,2,1,0:T(8,128)S(1)} collective-permute-done((f32[2,4,24,128]{3,2,1,0:T(8,128)S(1)}, f32[2,4,24,128]{3,2,1,0:T(8,128)S(1)}, u32[]{:S(2)}, u32[]{:S(2)}) %collective-permute-start.18) | collective-permute-done | bytes 98336 | tf_op jit(solution)/shard_map/ppermute | solution.py:478
  128.2 0.0 collective-permute-done.19.refs_3_
  128.2 0.0 collective-permute-done.20.refs_5_
  128.2 0.0 collective-permute-done.21.refs_6_
  128.2 0.0 collective-permute-done.22.refs_7_
  128.2 0.7 collective-permute-start.23
  128.9 18.0 %all_to_all.11 = f32[256,1,128]{2,1,0:T(1,128)S(1)} all-to-all(f32[256,1,128]{2,1,0:T(1,128)S(1)} %bitcast.10), channel_id=1, replica_groups=mesh['gx'=4,'gy'=8,'gz'=8] {'gz','gy','gx'}, dimensions={0} | all-to-all | bytes 262144 | tf_op jit(solution)/shard_map/all_to_all | solution.py:549
  146.9 0.0 collective-permute-done.23.passed
  146.9 1.5 %finish.1 = (f32[32,64,128]{2,1,0:T(8,128)}, f32[1,32]{1,0:T(1,128)}, f32[1,32]{1,0:T(1,128)}) custom-call(s32[3]{0:T(128)S(1)} %pad_add_fusion.idx, f32[256,128]{1,0:T(8,128)S(1)} %bitcast.9, f32[4,4,64,128]{3,2,1,0:T(8,128)S(1)} %collective-permute-done.23.passed, f32[2,4,24,128]{3,2,1,0:T(8,128)S(1)} %get-tuple-element.62.refs_0_, ...), custom_call_target="tpu_custom_call" | custom-call | tf_op jit(solution)/shard_map/finish/pallas_call | solution.py:455
  (1 shorter events, 0.0 us)
Async XLA Ops:
  3.0 9.5 %collective-permute-start.1 = (f32[72,1024]{1,0:T(8,128)S(1)}, f32[72,1024]{1,0:T(8,128)S(1)}, u32[]{:S(2)}, u32[]{:S(2)}) collective-permute-start(f32[72,1024]{1,0:T(8,128)S(1)} %get-tuple-element.42), channel_id=1, source_target_pairs={{0,64},{64,128},{128,192},{192,0},{1,65},{65,129},{129,193},{193,1... | collective-permute-start | bytes 884744 | tf_op jit(solution)/shard_map/ppermute | solution.py:496
  7.4 47.6 %collective-permute-start = (f32[168,1024]{1,0:T(8,128)S(1)}, f32[168,1024]{1,0:T(8,128)S(1)}, u32[]{:S(2)}, u32[]{:S(2)}) collective-permute-start(f32[168,1024]{1,0:T(8,128)S(1)} %get-tuple-element.41), channel_id=1, source_target_pairs={{0,64},{64,128},{128,192},{192,0},{1,65},{65,129},{129,193},{193,1... | collective-permute-start | bytes 2064392 | tf_op jit(solution)/shard_map/ppermute | solution.py:496
  8.7 51.5 %collective-permute-start.3 = (f32[168,1024]{1,0:T(8,128)S(1)}, f32[168,1024]{1,0:T(8,128)S(1)}, u32[]{:S(2)}, u32[]{:S(2)}) collective-permute-start(f32[168,1024]{1,0:T(8,128)S(1)} %get-tuple-element.44), channel_id=1, source_target_pairs={{0,128},{64,192},{128,0},{192,64},{1,129},{65,193},{129,1},{193,65... | collective-permute-start | bytes 2064392 | tf_op jit(solution)/shard_map/ppermute | solution.py:496
  10.0 51.7 %collective-permute-start.6 = (f32[168,1024]{1,0:T(8,128)S(1)}, f32[168,1024]{1,0:T(8,128)S(1)}, u32[]{:S(2)}, u32[]{:S(2)}) collective-permute-start(f32[168,1024]{1,0:T(8,128)S(1)} %get-tuple-element.47), channel_id=1, source_target_pairs={{0,192},{64,0},{128,64},{192,128},{1,193},{65,1},{129,65},{193,129... | collective-permute-start | bytes 2064392 | tf_op jit(solution)/shard_map/ppermute | solution.py:496
  12.0 37.8 %collective-permute-start.4 = (f32[72,1024]{1,0:T(8,128)S(1)}, f32[72,1024]{1,0:T(8,128)S(1)}, u32[]{:S(2)}, u32[]{:S(2)}) collective-permute-start(f32[72,1024]{1,0:T(8,128)S(1)} %get-tuple-element.45), channel_id=1, source_target_pairs={{0,128},{64,192},{128,0},{192,64},{1,129},{65,193},{129,1},{193,65... | collective-permute-start | bytes 884744 | tf_op jit(solution)/shard_map/ppermute | solution.py:496
  12.5 40.5 %collective-permute-start.7 = (f32[72,1024]{1,0:T(8,128)S(1)}, f32[72,1024]{1,0:T(8,128)S(1)}, u32[]{:S(2)}, u32[]{:S(2)}) collective-permute-start(f32[72,1024]{1,0:T(8,128)S(1)} %get-tuple-element.48), channel_id=1, source_target_pairs={{0,192},{64,0},{128,64},{192,128},{1,193},{65,1},{129,65},{193,129... | collective-permute-start | bytes 884744 | tf_op jit(solution)/shard_map/ppermute | solution.py:496
  49.8 18.8 %collective-permute-start.2 = (f32[96,1024]{1,0:T(8,128)S(1)}, f32[96,1024]{1,0:T(8,128)S(1)}, u32[]{:S(2)}, u32[]{:S(2)}) collective-permute-start(f32[96,1024]{1,0:T(8,128)S(1)} %get-tuple-element.43), channel_id=1, source_target_pairs={{0,64},{64,128},{128,192},{192,0},{1,65},{65,129},{129,193},{193,1... | collective-permute-start | bytes 1179656 | tf_op jit(solution)/shard_map/ppermute | solution.py:496
  53.0 18.0 %collective-permute-start.5 = (f32[96,1024]{1,0:T(8,128)S(1)}, f32[96,1024]{1,0:T(8,128)S(1)}, u32[]{:S(2)}, u32[]{:S(2)}) collective-permute-start(f32[96,1024]{1,0:T(8,128)S(1)} %get-tuple-element.46), channel_id=1, source_target_pairs={{0,128},{64,192},{128,0},{192,64},{1,129},{65,193},{129,1},{193,65... | collective-permute-start | bytes 1179656 | tf_op jit(solution)/shard_map/ppermute | solution.py:496
  55.0 19.2 %collective-permute-start.8 = (f32[96,1024]{1,0:T(8,128)S(1)}, f32[96,1024]{1,0:T(8,128)S(1)}, u32[]{:S(2)}, u32[]{:S(2)}) collective-permute-start(f32[96,1024]{1,0:T(8,128)S(1)} %get-tuple-element.49), channel_id=1, source_target_pairs={{0,192},{64,0},{128,64},{192,128},{1,193},{65,1},{129,65},{193,129... | collective-permute-start | bytes 1179656 | tf_op jit(solution)/shard_map/ppermute | solution.py:496
  60.2 14.0 %collective-permute-start.10 = (f32[72,1024]{1,0:T(8,128)S(1)}, f32[72,1024]{1,0:T(8,128)S(1)}, u32[]{:S(2)}, u32[]{:S(2)}) collective-permute-start(f32[72,1024]{1,0:T(8,128)S(1)} %get-tuple-element.51), channel_id=1, source_target_pairs={{0,8},{16,24},{32,40},{48,56},{1,9},{17,25},{33,41},{49,57},{2,10}... | collective-permute-start | bytes 884744 | tf_op jit(solution)/shard_map/ppermute | solution.py:513
  61.7 12.5 %collective-permute-start.12 = (f32[72,1024]{1,0:T(8,128)S(1)}, f32[72,1024]{1,0:T(8,128)S(1)}, u32[]{:S(2)}, u32[]{:S(2)}) collective-permute-start(f32[72,1024]{1,0:T(8,128)S(1)} %get-tuple-element.53), channel_id=1, source_target_pairs={{8,16},{24,32},{40,48},{56,1},{9,17},{25,33},{41,49},{57,2},{10,18... | collective-permute-start | bytes 884744 | tf_op jit(solution)/shard_map/ppermute | solution.py:513
  68.6 5.6 %collective-permute-start.9 = (f32[72,1024]{1,0:T(8,128)S(1)}, f32[72,1024]{1,0:T(8,128)S(1)}, u32[]{:S(2)}, u32[]{:S(2)}) collective-permute-start(f32[72,1024]{1,0:T(8,128)S(1)} %get-tuple-element.50), channel_id=1, source_target_pairs={{0,8},{16,24},{32,40},{48,56},{1,9},{17,25},{33,41},{49,57},{2,10}... | collective-permute-start | bytes 884744 | tf_op jit(solution)/shard_map/ppermute | solution.py:513
  71.0 6.1 %collective-permute-start.11 = (f32[72,1024]{1,0:T(8,128)S(1)}, f32[72,1024]{1,0:T(8,128)S(1)}, u32[]{:S(2)}, u32[]{:S(2)}) collective-permute-start(f32[72,1024]{1,0:T(8,128)S(1)} %get-tuple-element.52), channel_id=1, source_target_pairs={{8,16},{24,32},{40,48},{56,1},{9,17},{25,33},{41,49},{57,2},{10,18... | collective-permute-start | bytes 884744 | tf_op jit(solution)/shard_map/ppermute | solution.py:513
  78.8 21.7 %collective-permute-start.14 = (f32[40,1024]{1,0:T(8,128)S(1)}, f32[40,1024]{1,0:T(8,128)S(1)}, u32[]{:S(2)}, u32[]{:S(2)}) collective-permute-start(f32[40,1024]{1,0:T(8,128)S(1)} %get-tuple-element.57), channel_id=1, source_target_pairs={{0,8},{16,24},{32,40},{48,56},{1,9},{17,25},{33,41},{49,57},{2,10}... | collective-permute-start | bytes 491528 | tf_op jit(solution)/shard_map/ppermute | solution.py:513
  85.6 14.9 %collective-permute-start.16 = (f32[40,1024]{1,0:T(8,128)S(1)}, f32[40,1024]{1,0:T(8,128)S(1)}, u32[]{:S(2)}, u32[]{:S(2)}) collective-permute-start(f32[40,1024]{1,0:T(8,128)S(1)} %get-tuple-element.59), channel_id=1, source_target_pairs={{8,16},{24,32},{40,48},{56,1},{9,17},{25,33},{41,49},{57,2},{10,18... | collective-permute-start | bytes 491528 | tf_op jit(solution)/shard_map/ppermute | solution.py:513
  87.8 6.2 %collective-permute-start.13 = (f32[24,1024]{1,0:T(8,128)S(1)}, f32[24,1024]{1,0:T(8,128)S(1)}, u32[]{:S(2)}, u32[]{:S(2)}) collective-permute-start(f32[24,1024]{1,0:T(8,128)S(1)} %get-tuple-element.56), channel_id=1, source_target_pairs={{0,8},{16,24},{32,40},{48,56},{1,9},{17,25},{33,41},{49,57},{2,10}... | collective-permute-start | bytes 294920 | tf_op jit(solution)/shard_map/ppermute | solution.py:513
  93.0 4.0 %collective-permute-start.15 = (f32[24,1024]{1,0:T(8,128)S(1)}, f32[24,1024]{1,0:T(8,128)S(1)}, u32[]{:S(2)}, u32[]{:S(2)}) collective-permute-start(f32[24,1024]{1,0:T(8,128)S(1)} %get-tuple-element.58), channel_id=1, source_target_pairs={{8,16},{24,32},{40,48},{56,1},{9,17},{25,33},{41,49},{57,2},{10,18... | collective-permute-start | bytes 294920 | tf_op jit(solution)/shard_map/ppermute | solution.py:513
  98.7 8.1 %collective-permute-start.17 = (f32[2,4,24,128]{3,2,1,0:T(8,128)S(1)}, f32[2,4,24,128]{3,2,1,0:T(8,128)S(1)}, u32[]{:S(2)}, u32[]{:S(2)}) collective-permute-start(f32[2,4,24,128]{3,2,1,0:T(8,128)S(1)} %get-tuple-element.63), channel_id=1, source_target_pairs={{0,16},{8,24},{16,0},{24,8},{32,48},{40,56},{48,32},{56,40},{1,17}... | collective-permute-start | bytes 294920 | tf_op jit(solution)/shard_map/ppermute | solution.py:478
  102.9 25.3 %collective-permute-start.20 = (f32[2,4,40,128]{3,2,1,0:T(8,128)S(1)}, f32[2,4,40,128]{3,2,1,0:T(8,128)S(1)}, u32[]{:S(2)}, u32[]{:S(2)}) collective-permute-start(f32[2,4,40,128]{3,2,1,0:T(8,128)S(1)} %get-tuple-element.67), channel_id=1, source_target_pairs={{0,16},{8,24},{16,0},{24,8},{32,48},{40,56},{48,32},{56,40},{1,17}... | collective-permute-start | bytes 491528 | tf_op jit(solution)/shard_map/ppermute | solution.py:478
  104.4 23.7 %collective-permute-start.21 = (f32[2,4,40,128]{3,2,1,0:T(8,128)S(1)}, f32[2,4,40,128]{3,2,1,0:T(8,128)S(1)}, u32[]{:S(2)}, u32[]{:S(2)}) collective-permute-start(f32[2,4,40,128]{3,2,1,0:T(8,128)S(1)} %get-tuple-element.68), channel_id=1, source_target_pairs={{0,32},{8,40},{16,48},{24,56},{32,0},{40,8},{48,16},{56,24},{1,33}... | collective-permute-start | bytes 491528 | tf_op jit(solution)/shard_map/ppermute | solution.py:478
  104.4 23.7 %collective-permute-start.22 = (f32[2,4,40,128]{3,2,1,0:T(8,128)S(1)}, f32[2,4,40,128]{3,2,1,0:T(8,128)S(1)}, u32[]{:S(2)}, u32[]{:S(2)}) collective-permute-start(f32[2,4,40,128]{3,2,1,0:T(8,128)S(1)} %get-tuple-element.69), channel_id=1, source_target_pairs={{0,48},{8,56},{16,32},{24,40},{32,16},{40,24},{48,0},{56,8},{1,49}... | collective-permute-start | bytes 491528 | tf_op jit(solution)/shard_map/ppermute | solution.py:478
  106.6 21.5 %collective-permute-start.18 = (f32[2,4,24,128]{3,2,1,0:T(8,128)S(1)}, f32[2,4,24,128]{3,2,1,0:T(8,128)S(1)}, u32[]{:S(2)}, u32[]{:S(2)}) collective-permute-start(f32[2,4,24,128]{3,2,1,0:T(8,128)S(1)} %get-tuple-element.64), channel_id=1, source_target_pairs={{0,32},{8,40},{16,48},{24,56},{32,0},{40,8},{48,16},{56,24},{1,33}... | collective-permute-start | bytes 294920 | tf_op jit(solution)/shard_map/ppermute | solution.py:478
  106.8 21.3 %collective-permute-start.19 = (f32[2,4,24,128]{3,2,1,0:T(8,128)S(1)}, f32[2,4,24,128]{3,2,1,0:T(8,128)S(1)}, u32[]{:S(2)}, u32[]{:S(2)}) collective-permute-start(f32[2,4,24,128]{3,2,1,0:T(8,128)S(1)} %get-tuple-element.65), channel_id=1, source_target_pairs={{0,48},{8,56},{16,32},{24,40},{32,16},{40,24},{48,0},{56,8},{1,49}... | collective-permute-start | bytes 294920 | tf_op jit(solution)/shard_map/ppermute | solution.py:478
  128.2 18.7 %collective-permute-start.23 = (f32[4,4,64,128]{3,2,1,0:T(8,128)S(1)}, f32[4,4,64,128]{3,2,1,0:T(8,128)S(1)}, u32[]{:S(2)}, u32[]{:S(2)}) collective-permute-start(f32[4,4,64,128]{3,2,1,0:T(8,128)S(1)} %pass_on.1), channel_id=1, source_target_pairs={{0,8},{8,0},{16,24},{24,16},{32,40},{40,32},{48,56},{56,48},{1,9},... | collective-permute-start | bytes 1572872 | tf_op jit(solution)/shard_map/ppermute | solution.py:552

commit v2 on v1

--- a/solution.py
+++ b/solution.py
@@ -303,7 +303,7 @@
     *slots, even, odd, half, half_even, half_odd, early, pieces, refs = grouped(
         refs, [given[0]] * quarters + [given[1]] * 2 + [len(halves)] * 3 + [before, blocks // 2]
     )
-    total_ref, e, k, u, result, totals = refs
+    total_ref, e, k, u, result, totals, *held = refs
     me, my = idx[0], idx[1]
     outer = [beyond(plane) for plane in end_planes(idx, quarters)]
     ends = list(zip(outer, (even, odd)))
@@ -339,13 +339,18 @@
     found = jnp.zeros((ROWS, LANES), F32)
     for plane in range(quarters):
         found = jnp.where(lane == my * quarters + plane, jnp.sum(totals[plane]), found)
+    if before:
+        held, sem = held
+        held[...] = jnp.broadcast_to((early[0][...] + found)[:1], held.shape)
+        sending = pltpu.make_async_copy(held, total_ref, sem)
+        sending.start()
+    else:
+        total_ref[...] = found
     for n in range(blocks):
         lanes = pl.ds(pl.multiple_of(jnp.bitwise_xor(my, n) * LANES, LANES), LANES)
         pieces[n // 2][n % 2] = result[:, :, lanes]
     if before:
-        total_ref[...] = jnp.broadcast_to((early[0][...] + found)[:1], total_ref.shape)
-    else:
-        total_ref[...] = found
+        sending.wait()
 
 
 def second_step(
@@ -364,9 +369,10 @@
         ),
         out_shape=shapes,
         in_specs=[SMEM] + [VMEM] * len(flat),
-        out_specs=[VMEM] * len(shapes),
+        out_specs=[VMEM] * (len(shapes) - 1) + [ANY if before else VMEM],
         scratch_shapes=scratch(quarters, window[1] - window[0], width)
-        + [pltpu.VMEM((quarters, size, width), F32), pltpu.VMEM((quarters, ROWS, LANES), F32)],
+        + [pltpu.VMEM((quarters, size, width), F32), pltpu.VMEM((quarters, ROWS, LANES), F32)]
+        + ([pltpu.VMEM((count, LANES), F32), pltpu.SemaphoreType.DMA] if before else []),
         compiler_params=params(),
         name="second_step",
     )(idx, *flat)

time: 149 us -> 149 us (level)
  no operation moved by 1% of the time
where the time goes in v2:
time: 149 us
  waiting for transfers between devices  71 us (48%)
  starting transfers between devices  39.6 us (27%)
  Pallas kernels  19.3 us (13%)
  blocking collectives  18 us (12%)
    ppermute x9, waiting for transfers between devices, both_steps(): lax.ppermute(sent[slot][part], 'gx', shift(quarters, slot))  45 us
    ppermute x8, starting transfers between devices, exchanged(): got.append(lax.ppermute(value, ('gy', 'gz'), pairs))  19.1 us
    ppermute x6, waiting for transfers between devices, over_chips(): got.append(lax.ppermute(pair, 'gy', where))  19 us
    all_to_all x1, blocking collectives, both_steps(): found = everyone(sums, ('gz', 'gy', 'gx'), 0, 0)  18 us
    ppermute x9, starting transfers between devices, both_steps(): lax.ppermute(sent[slot][part], 'gx', shift(quarters, slot))  13.5 us
    ppermute x8, waiting for transfers between devices, exchanged(): got.append(lax.ppermute(value, ('gy', 'gz'), pairs))  7 us
    pallas_call x3, Pallas kernels, pack(): pl.pallas_call(functools.partial(pack_body, quarters, rows, cut, slots, p...  6.58 us
    ppermute x6, starting transfers between devices, over_chips(): got.append(lax.ppermute(pair, 'gy', where))  6.35 us
  transfers between devices with their start and end apart: 24, of which 8 were waited for; matrix products, arithmetic and copies ran while one was open for 0% of the time, Pallas kernels for 9%

profile of v2, /device:TPU:1, one launch (start us, length us, event | category | flops | bytes accessed | tf_op | source)
XLA Modules:
  0.0 148.9 jit_solution(17776747950856373648)
XLA Ops:
  0.6 0.1 pad_add_fusion.idx
  0.7 2.3 %pack.5 = (f32[72,1024]{1,0:T(8,128)S(1)}, f32[96,1024]{1,0:T(8,128)S(1)}, f32[72,1024]{1,0:T(8,128)S(1)}, f32[96,1024]{1,0:T(8,128)S(1)}, f32[72,1024]{1,0:T(8,128)S(1)}, /*index=5*/f32[96,1024]{1,0:T(8,128)S(1)}) custom-call(s32[3]{0:T(128)S(1)} %pad_add_fusion.idx, f32[1,256,1024]{2,1,0:T(8,128)} %energy.5, f32[4,1,256,1024]{3,2,1,0:T(8,128)} %flow.5), custom_call_target="tpu_custom_call" | custom-call | tf_op jit(solution)/shard_map/pack/pallas_call | solution.py:117
  3.0 2.1 %collective-permute-start.1 = (f32[72,1024]{1,0:T(8,128)S(1)}, f32[72,1024]{1,0:T(8,128)S(1)}, u32[]{:S(2)}, u32[]{:S(2)}) collective-permute-start(f32[72,1024]{1,0:T(8,128)S(1)} %get-tuple-element.42), channel_id=1, source_target_pairs={{0,64},{64,128},{128,192},{192,0},{1,65},{65,129},{129,193},{193,1... | collective-permute-start | bytes 884744 | tf_op jit(solution)/shard_map/ppermute | solution.py:502
  5.1 2.3 %pack.4 = (f32[168,1024]{1,0:T(8,128)S(1)}, f32[168,1024]{1,0:T(8,128)S(1)}, f32[168,1024]{1,0:T(8,128)S(1)}) custom-call(s32[3]{0:T(128)S(1)} %pad_add_fusion.idx, f32[1,256,1024]{2,1,0:T(8,128)} %energy.5, f32[4,1,256,1024]{3,2,1,0:T(8,128)} %flow.5), custom_call_target="tpu_custom_call" | custom-call | tf_op jit(solution)/shard_map/pack/pallas_call | solution.py:117
  7.4 1.3 collective-permute-start
  8.7 1.3 collective-permute-start.3
  10.0 2.0 %collective-permute-start.6 = (f32[168,1024]{1,0:T(8,128)S(1)}, f32[168,1024]{1,0:T(8,128)S(1)}, u32[]{:S(2)}, u32[]{:S(2)}) collective-permute-start(f32[168,1024]{1,0:T(8,128)S(1)} %get-tuple-element.47), channel_id=1, source_target_pairs={{0,192},{64,0},{128,64},{192,128},{1,193},{65,1},{129,65},{193,129... | collective-permute-start | bytes 2064392 | tf_op jit(solution)/shard_map/ppermute | solution.py:502
  12.0 0.5 collective-permute-start.4
  12.5 0.0 collective-permute-done.1.refs_1_.refs_4_
  12.5 1.8 %collective-permute-start.7 = (f32[72,1024]{1,0:T(8,128)S(1)}, f32[72,1024]{1,0:T(8,128)S(1)}, u32[]{:S(2)}, u32[]{:S(2)}) collective-permute-start(f32[72,1024]{1,0:T(8,128)S(1)} %get-tuple-element.48), channel_id=1, source_target_pairs={{0,192},{64,0},{128,64},{192,128},{1,193},{65,1},{129,65},{193,129... | collective-permute-start | bytes 884744 | tf_op jit(solution)/shard_map/ppermute | solution.py:502
  14.3 35.5 %collective-permute-done.4.refs_2_.refs_7_ = f32[72,1024]{1,0:T(8,128)S(1)} collective-permute-done((f32[72,1024]{1,0:T(8,128)S(1)}, f32[72,1024]{1,0:T(8,128)S(1)}, u32[]{:S(2)}, u32[]{:S(2)}) %collective-permute-start.4) | collective-permute-done | bytes 294944 | tf_op jit(solution)/shard_map/ppermute | solution.py:502
  49.8 0.0 collective-permute-start.2
  49.8 3.2 %collective-permute-done.7.refs_3_.refs_10_ = f32[72,1024]{1,0:T(8,128)S(1)} collective-permute-done((f32[72,1024]{1,0:T(8,128)S(1)}, f32[72,1024]{1,0:T(8,128)S(1)}, u32[]{:S(2)}, u32[]{:S(2)}) %collective-permute-start.7) | collective-permute-done | bytes 294944 | tf_op jit(solution)/shard_map/ppermute | solution.py:502
  53.0 2.0 %collective-permute-start.5 = (f32[96,1024]{1,0:T(8,128)S(1)}, f32[96,1024]{1,0:T(8,128)S(1)}, u32[]{:S(2)}, u32[]{:S(2)}) collective-permute-start(f32[96,1024]{1,0:T(8,128)S(1)} %get-tuple-element.46), channel_id=1, source_target_pairs={{0,128},{64,192},{128,0},{192,64},{1,129},{65,193},{129,1},{193,65... | collective-permute-start | bytes 1179656 | tf_op jit(solution)/shard_map/ppermute | solution.py:502
  55.0 0.0 collective-permute-done.refs_1_.refs_3_
  55.0 2.5 %collective-permute-start.8 = (f32[96,1024]{1,0:T(8,128)S(1)}, f32[96,1024]{1,0:T(8,128)S(1)}, u32[]{:S(2)}, u32[]{:S(2)}) collective-permute-start(f32[96,1024]{1,0:T(8,128)S(1)} %get-tuple-element.49), channel_id=1, source_target_pairs={{0,192},{64,0},{128,64},{192,128},{1,193},{65,1},{129,65},{193,129... | collective-permute-start | bytes 1179656 | tf_op jit(solution)/shard_map/ppermute | solution.py:502
  57.5 2.0 %pack.3 = (f32[168,1024]{1,0:T(8,128)S(1)}, f32[72,1024]{1,0:T(8,128)S(1)}, f32[96,1024]{1,0:T(8,128)S(1)}) custom-call(s32[3]{0:T(128)S(1)} %pad_add_fusion.idx, f32[1,256,1024]{2,1,0:T(8,128)} %energy.5, f32[4,1,256,1024]{3,2,1,0:T(8,128)} %flow.5), custom_call_target="tpu_custom_call" | custom-call | tf_op jit(solution)/shard_map/pack/pallas_call | solution.py:117
  59.5 0.6 ends.3
  60.2 0.0 collective-permute-done.3.refs_2_.refs_6_
  60.2 1.5 %collective-permute-start.10 = (f32[72,1024]{1,0:T(8,128)S(1)}, f32[72,1024]{1,0:T(8,128)S(1)}, u32[]{:S(2)}, u32[]{:S(2)}) collective-permute-start(f32[72,1024]{1,0:T(8,128)S(1)} %get-tuple-element.51), channel_id=1, source_target_pairs={{0,8},{16,24},{32,40},{48,56},{1,9},{17,25},{33,41},{49,57},{2,10}... | collective-permute-start | bytes 884744 | tf_op jit(solution)/shard_map/ppermute | solution.py:519
  61.7 0.0 collective-permute-done.6.refs_3_.refs_9_
  61.7 1.6 %collective-permute-start.12 = (f32[72,1024]{1,0:T(8,128)S(1)}, f32[72,1024]{1,0:T(8,128)S(1)}, u32[]{:S(2)}, u32[]{:S(2)}) collective-permute-start(f32[72,1024]{1,0:T(8,128)S(1)} %get-tuple-element.53), channel_id=1, source_target_pairs={{8,16},{24,32},{40,48},{56,1},{9,17},{25,33},{41,49},{57,2},{10,18... | collective-permute-start | bytes 884744 | tf_op jit(solution)/shard_map/ppermute | solution.py:519
  63.3 0.6 ends.2
  64.0 4.6 %collective-permute-done.2.refs_5_ = f32[96,1024]{1,0:T(8,128)S(1)} collective-permute-done((f32[96,1024]{1,0:T(8,128)S(1)}, f32[96,1024]{1,0:T(8,128)S(1)}, u32[]{:S(2)}, u32[]{:S(2)}) %collective-permute-start.2) | collective-permute-done | bytes 393248 | tf_op jit(solution)/shard_map/ppermute | solution.py:502
  68.6 2.4 %collective-permute-start.9 = (f32[72,1024]{1,0:T(8,128)S(1)}, f32[72,1024]{1,0:T(8,128)S(1)}, u32[]{:S(2)}, u32[]{:S(2)}) collective-permute-start(f32[72,1024]{1,0:T(8,128)S(1)} %get-tuple-element.50), channel_id=1, source_target_pairs={{0,8},{16,24},{32,40},{48,56},{1,9},{17,25},{33,41},{49,57},{2,10}... | collective-permute-start | bytes 884744 | tf_op jit(solution)/shard_map/ppermute | solution.py:519
  71.0 0.0 collective-permute-done.5.refs_8_
  71.0 1.5 %collective-permute-start.11 = (f32[72,1024]{1,0:T(8,128)S(1)}, f32[72,1024]{1,0:T(8,128)S(1)}, u32[]{:S(2)}, u32[]{:S(2)}) collective-permute-start(f32[72,1024]{1,0:T(8,128)S(1)} %get-tuple-element.52), channel_id=1, source_target_pairs={{8,16},{24,32},{40,48},{56,1},{9,17},{25,33},{41,49},{57,2},{10,18... | collective-permute-start | bytes 884744 | tf_op jit(solution)/shard_map/ppermute | solution.py:519
  72.5 1.7 %collective-permute-done.8.refs_11_ = f32[96,1024]{1,0:T(8,128)S(1)} collective-permute-done((f32[96,1024]{1,0:T(8,128)S(1)}, f32[96,1024]{1,0:T(8,128)S(1)}, u32[]{:S(2)}, u32[]{:S(2)}) %collective-permute-start.8) | collective-permute-done | bytes 393248 | tf_op jit(solution)/shard_map/ppermute | solution.py:502
  74.2 0.0 collective-permute-done.10.refs_13_
  74.2 0.0 collective-permute-done.12.refs_15_
  74.2 0.0 collective-permute-done.9.refs_4_.refs_12_
  74.2 2.9 %collective-permute-done.11.refs_5_.refs_14_ = f32[72,1024]{1,0:T(8,128)S(1)} collective-permute-done((f32[72,1024]{1,0:T(8,128)S(1)}, f32[72,1024]{1,0:T(8,128)S(1)}, u32[]{:S(2)}, u32[]{:S(2)}) %collective-permute-start.11) | collective-permute-done | bytes 294944 | tf_op jit(solution)/shard_map/ppermute | solution.py:519
  77.1 1.7 %first_step.4 = (f32[2,48,1024]{2,1,0:T(8,128)S(1)}, f32[40,1024]{1,0:T(8,128)S(1)}, f32[40,1024]{1,0:T(8,128)S(1)}) custom-call(s32[3]{0:T(128)S(1)} %pad_add_fusion.idx, f32[168,1024]{1,0:T(8,128)S(1)} %get-tuple-element.38.refs_0_, f32[72,1024]{1,0:T(8,128)S(1)} %get-tuple-element.39.refs_0_.refs_1_, f32[96,1024]{1,0:T(8,128)S(1)} %get-tuple-element.40.refs_2_, ...), custom_call_target="tpu_custom_call" | custom-call | tf_op jit(solution)/shard_map/first_step/pallas_call | solution.py:289
  78.8 6.8 %collective-permute-start.14 = (f32[40,1024]{1,0:T(8,128)S(1)}, f32[40,1024]{1,0:T(8,128)S(1)}, u32[]{:S(2)}, u32[]{:S(2)}) collective-permute-start(f32[40,1024]{1,0:T(8,128)S(1)} %get-tuple-element.57), channel_id=1, source_target_pairs={{0,8},{16,24},{32,40},{48,56},{1,9},{17,25},{33,41},{49,57},{2,10}... | collective-permute-start | bytes 491528 | tf_op jit(solution)/shard_map/ppermute | solution.py:519
  85.6 0.0 collective-permute-start.16
  85.6 2.2 %first_step.3 = (f32[4,40,1024]{2,1,0:T(8,128)S(1)}, f32[24,1024]{1,0:T(8,128)S(1)}, f32[24,1024]{1,0:T(8,128)S(1)}) custom-call(s32[3]{0:T(128)S(1)} %pad_add_fusion.idx, f32[168,1024]{1,0:T(8,128)S(1)} %get-tuple-element.38.refs_0_, f32[168,1024]{1,0:T(8,128)S(1)} %collective-permute-done.refs_1_.refs_3_, ...), custom_call_target="tpu_custom_call" | custom-call | tf_op jit(solution)/shard_map/first_step/pallas_call | solution.py:289
  87.8 5.2 %collective-permute-start.13 = (f32[24,1024]{1,0:T(8,128)S(1)}, f32[24,1024]{1,0:T(8,128)S(1)}, u32[]{:S(2)}, u32[]{:S(2)}) collective-permute-start(f32[24,1024]{1,0:T(8,128)S(1)} %get-tuple-element.56), channel_id=1, source_target_pairs={{0,8},{16,24},{32,40},{48,56},{1,9},{17,25},{33,41},{49,57},{2,10}... | collective-permute-start | bytes 294920 | tf_op jit(solution)/shard_map/ppermute | solution.py:519
  93.0 0.0 collective-permute-start.15
  93.0 0.9 collective-permute-done.13.refs_7_.refs_19_
  93.9 3.1 %collective-permute-done.15.refs_8_.refs_22_ = f32[24,1024]{1,0:T(8,128)S(1)} collective-permute-done((f32[24,1024]{1,0:T(8,128)S(1)}, f32[24,1024]{1,0:T(8,128)S(1)}, u32[]{:S(2)}, u32[]{:S(2)}) %collective-permute-start.15) | collective-permute-done | bytes 98336 | tf_op jit(solution)/shard_map/ppermute | solution.py:519
  97.0 1.7 %second_step.2 = (f32[2,4,24,128]{3,2,1,0:T(8,128)S(1)}, f32[2,4,24,128]{3,2,1,0:T(8,128)S(1)}, f32[2,4,24,128]{3,2,1,0:T(8,128)S(1)}, f32[2,4,24,128]{3,2,1,0:T(8,128)S(1)}, f32[8,128]{1,0:T(8,128)S(1)}) custom-call(s32[3]{0:T(128)S(1)} %pad_add_fusion.idx, f32[168,1024]{1,0:T(8,128)S(1)} %get-tuple-element.38.refs_0_, ...), custom_call_target="tpu_custom_call" | custom-call | tf_op jit(solution)/shard_map/second_step/pallas_call | solution.py:366
  98.7 0.1 collective-permute-start.17
  98.8 1.7 %first_step.5.refs_18_ = f32[2,48,1024]{2,1,0:T(8,128)S(1)} custom-call(s32[3]{0:T(128)S(1)} %pad_add_fusion.idx, f32[168,1024]{1,0:T(8,128)S(1)} %get-tuple-element.38.refs_0_, f32[72,1024]{1,0:T(8,128)S(1)} %get-tuple-element.39.refs_0_.refs_1_, f32[96,1024]{1,0:T(8,128)S(1)} %get-tuple-element.40.refs_2_, ...), custom_call_target="tpu_custom_call" | custom-call | tf_op jit(solution)/shard_map/first_step/pallas_call | solution.py:289
  100.5 0.0 collective-permute-done.14.refs_20_.refs_21_
  100.5 0.0 collective-permute-done.16.refs_23_.refs_24_
  100.5 2.7 %second_step.3 = (f32[2,4,40,128]{3,2,1,0:T(8,128)S(1)}, f32[2,4,40,128]{3,2,1,0:T(8,128)S(1)}, f32[2,4,40,128]{3,2,1,0:T(8,128)S(1)}, f32[2,4,40,128]{3,2,1,0:T(8,128)S(1)}, f32[256,128]{1,0:T(8,128)S(1)}) custom-call(s32[3]{0:T(128)S(1)} %pad_add_fusion.idx, f32[168,1024]{1,0:T(8,128)S(1)} %get-tuple-element.38.refs_0_, ...), custom_call_target="tpu_custom_call" | custom-call | tf_op jit(solution)/shard_map/second_step/pallas_call | solution.py:366
  103.2 1.5 %collective-permute-start.20 = (f32[2,4,40,128]{3,2,1,0:T(8,128)S(1)}, f32[2,4,40,128]{3,2,1,0:T(8,128)S(1)}, u32[]{:S(2)}, u32[]{:S(2)}) collective-permute-start(f32[2,4,40,128]{3,2,1,0:T(8,128)S(1)} %get-tuple-element.67), channel_id=1, source_target_pairs={{0,16},{8,24},{16,0},{24,8},{32,48},{40,56},{48,32},{56,40},{1,17}... | collective-permute-start | bytes 491528 | tf_op jit(solution)/shard_map/ppermute | solution.py:484
  104.7 0.0 collective-permute-start.21
  104.7 2.2 %collective-permute-start.22 = (f32[2,4,40,128]{3,2,1,0:T(8,128)S(1)}, f32[2,4,40,128]{3,2,1,0:T(8,128)S(1)}, u32[]{:S(2)}, u32[]{:S(2)}) collective-permute-start(f32[2,4,40,128]{3,2,1,0:T(8,128)S(1)} %get-tuple-element.69), channel_id=1, source_target_pairs={{0,48},{8,56},{16,32},{24,40},{32,16},{40,24},{48,0},{56,8},{1,49}... | collective-permute-start | bytes 491528 | tf_op jit(solution)/shard_map/ppermute | solution.py:484
  106.9 0.2 collective-permute-start.18
  107.1 0.0 collective-permute-done.17.refs_1_
  107.1 2.4 %collective-permute-start.19 = (f32[2,4,24,128]{3,2,1,0:T(8,128)S(1)}, f32[2,4,24,128]{3,2,1,0:T(8,128)S(1)}, u32[]{:S(2)}, u32[]{:S(2)}) collective-permute-start(f32[2,4,24,128]{3,2,1,0:T(8,128)S(1)} %get-tuple-element.65), channel_id=1, source_target_pairs={{0,48},{8,56},{16,32},{24,40},{32,16},{40,24},{48,0},{56,8},{1,49}... | collective-permute-start | bytes 294920 | tf_op jit(solution)/shard_map/ppermute | solution.py:484
  109.5 19.0 %collective-permute-done.18.refs_2_ = f32[2,4,24,128]{3,2,1,0:T(8,128)S(1)} collective-permute-done((f32[2,4,24,128]{3,2,1,0:T(8,128)S(1)}, f32[2,4,24,128]{3,2,1,0:T(8,128)S(1)}, u32[]{:S(2)}, u32[]{:S(2)}) %collective-permute-start.18) | collective-permute-done | bytes 98336 | tf_op jit(solution)/shard_map/ppermute | solution.py:484
  128.5 0.0 collective-permute-done.19.refs_3_
  128.5 0.0 collective-permute-done.20.refs_5_
  128.5 0.0 collective-permute-done.21.refs_6_
  128.5 0.0 collective-permute-done.22.refs_7_
  128.5 0.7 collective-permute-start.23
  129.2 18.0 %all_to_all.11 = f32[256,1,128]{2,1,0:T(1,128)S(1)} all-to-all(f32[256,1,128]{2,1,0:T(1,128)S(1)} %bitcast.10), channel_id=1, replica_groups=mesh['gx'=4,'gy'=8,'gz'=8] {'gz','gy','gx'}, dimensions={0} | all-to-all | bytes 262144 | tf_op jit(solution)/shard_map/all_to_all | solution.py:555
  147.2 0.0 collective-permute-done.23.passed
  147.3 1.5 %finish.1 = (f32[32,64,128]{2,1,0:T(8,128)}, f32[1,32]{1,0:T(1,128)}, f32[1,32]{1,0:T(1,128)}) custom-call(s32[3]{0:T(128)S(1)} %pad_add_fusion.idx, f32[256,128]{1,0:T(8,128)S(1)} %bitcast.9, f32[4,4,64,128]{3,2,1,0:T(8,128)S(1)} %collective-permute-done.23.passed, f32[2,4,24,128]{3,2,1,0:T(8,128)S(1)} %get-tuple-element.62.refs_0_, ...), custom_call_target="tpu_custom_call" | custom-call | tf_op jit(solution)/shard_map/finish/pallas_call | solution.py:461
  (1 shorter events, 0.0 us)
Async XLA Ops:
  3.0 9.5 %collective-permute-start.1 = (f32[72,1024]{1,0:T(8,128)S(1)}, f32[72,1024]{1,0:T(8,128)S(1)}, u32[]{:S(2)}, u32[]{:S(2)}) collective-permute-start(f32[72,1024]{1,0:T(8,128)S(1)} %get-tuple-element.42), channel_id=1, source_target_pairs={{0,64},{64,128},{128,192},{192,0},{1,65},{65,129},{129,193},{193,1... | collective-permute-start | bytes 884744 | tf_op jit(solution)/shard_map/ppermute | solution.py:502
  7.4 47.6 %collective-permute-start = (f32[168,1024]{1,0:T(8,128)S(1)}, f32[168,1024]{1,0:T(8,128)S(1)}, u32[]{:S(2)}, u32[]{:S(2)}) collective-permute-start(f32[168,1024]{1,0:T(8,128)S(1)} %get-tuple-element.41), channel_id=1, source_target_pairs={{0,64},{64,128},{128,192},{192,0},{1,65},{65,129},{129,193},{193,1... | collective-permute-start | bytes 2064392 | tf_op jit(solution)/shard_map/ppermute | solution.py:502
  8.7 51.5 %collective-permute-start.3 = (f32[168,1024]{1,0:T(8,128)S(1)}, f32[168,1024]{1,0:T(8,128)S(1)}, u32[]{:S(2)}, u32[]{:S(2)}) collective-permute-start(f32[168,1024]{1,0:T(8,128)S(1)} %get-tuple-element.44), channel_id=1, source_target_pairs={{0,128},{64,192},{128,0},{192,64},{1,129},{65,193},{129,1},{193,65... | collective-permute-start | bytes 2064392 | tf_op jit(solution)/shard_map/ppermute | solution.py:502
  10.0 51.7 %collective-permute-start.6 = (f32[168,1024]{1,0:T(8,128)S(1)}, f32[168,1024]{1,0:T(8,128)S(1)}, u32[]{:S(2)}, u32[]{:S(2)}) collective-permute-start(f32[168,1024]{1,0:T(8,128)S(1)} %get-tuple-element.47), channel_id=1, source_target_pairs={{0,192},{64,0},{128,64},{192,128},{1,193},{65,1},{129,65},{193,129... | collective-permute-start | bytes 2064392 | tf_op jit(solution)/shard_map/ppermute | solution.py:502
  12.0 37.8 %collective-permute-start.4 = (f32[72,1024]{1,0:T(8,128)S(1)}, f32[72,1024]{1,0:T(8,128)S(1)}, u32[]{:S(2)}, u32[]{:S(2)}) collective-permute-start(f32[72,1024]{1,0:T(8,128)S(1)} %get-tuple-element.45), channel_id=1, source_target_pairs={{0,128},{64,192},{128,0},{192,64},{1,129},{65,193},{129,1},{193,65... | collective-permute-start | bytes 884744 | tf_op jit(solution)/shard_map/ppermute | solution.py:502
  12.5 40.5 %collective-permute-start.7 = (f32[72,1024]{1,0:T(8,128)S(1)}, f32[72,1024]{1,0:T(8,128)S(1)}, u32[]{:S(2)}, u32[]{:S(2)}) collective-permute-start(f32[72,1024]{1,0:T(8,128)S(1)} %get-tuple-element.48), channel_id=1, source_target_pairs={{0,192},{64,0},{128,64},{192,128},{1,193},{65,1},{129,65},{193,129... | collective-permute-start | bytes 884744 | tf_op jit(solution)/shard_map/ppermute | solution.py:502
  49.8 18.8 %collective-permute-start.2 = (f32[96,1024]{1,0:T(8,128)S(1)}, f32[96,1024]{1,0:T(8,128)S(1)}, u32[]{:S(2)}, u32[]{:S(2)}) collective-permute-start(f32[96,1024]{1,0:T(8,128)S(1)} %get-tuple-element.43), channel_id=1, source_target_pairs={{0,64},{64,128},{128,192},{192,0},{1,65},{65,129},{129,193},{193,1... | collective-permute-start | bytes 1179656 | tf_op jit(solution)/shard_map/ppermute | solution.py:502
  53.0 18.0 %collective-permute-start.5 = (f32[96,1024]{1,0:T(8,128)S(1)}, f32[96,1024]{1,0:T(8,128)S(1)}, u32[]{:S(2)}, u32[]{:S(2)}) collective-permute-start(f32[96,1024]{1,0:T(8,128)S(1)} %get-tuple-element.46), channel_id=1, source_target_pairs={{0,128},{64,192},{128,0},{192,64},{1,129},{65,193},{129,1},{193,65... | collective-permute-start | bytes 1179656 | tf_op jit(solution)/shard_map/ppermute | solution.py:502
  55.0 19.2 %collective-permute-start.8 = (f32[96,1024]{1,0:T(8,128)S(1)}, f32[96,1024]{1,0:T(8,128)S(1)}, u32[]{:S(2)}, u32[]{:S(2)}) collective-permute-start(f32[96,1024]{1,0:T(8,128)S(1)} %get-tuple-element.49), channel_id=1, source_target_pairs={{0,192},{64,0},{128,64},{192,128},{1,193},{65,1},{129,65},{193,129... | collective-permute-start | bytes 1179656 | tf_op jit(solution)/shard_map/ppermute | solution.py:502
  60.2 14.0 %collective-permute-start.10 = (f32[72,1024]{1,0:T(8,128)S(1)}, f32[72,1024]{1,0:T(8,128)S(1)}, u32[]{:S(2)}, u32[]{:S(2)}) collective-permute-start(f32[72,1024]{1,0:T(8,128)S(1)} %get-tuple-element.51), channel_id=1, source_target_pairs={{0,8},{16,24},{32,40},{48,56},{1,9},{17,25},{33,41},{49,57},{2,10}... | collective-permute-start | bytes 884744 | tf_op jit(solution)/shard_map/ppermute | solution.py:519
  61.7 12.5 %collective-permute-start.12 = (f32[72,1024]{1,0:T(8,128)S(1)}, f32[72,1024]{1,0:T(8,128)S(1)}, u32[]{:S(2)}, u32[]{:S(2)}) collective-permute-start(f32[72,1024]{1,0:T(8,128)S(1)} %get-tuple-element.53), channel_id=1, source_target_pairs={{8,16},{24,32},{40,48},{56,1},{9,17},{25,33},{41,49},{57,2},{10,18... | collective-permute-start | bytes 884744 | tf_op jit(solution)/shard_map/ppermute | solution.py:519
  68.6 5.6 %collective-permute-start.9 = (f32[72,1024]{1,0:T(8,128)S(1)}, f32[72,1024]{1,0:T(8,128)S(1)}, u32[]{:S(2)}, u32[]{:S(2)}) collective-permute-start(f32[72,1024]{1,0:T(8,128)S(1)} %get-tuple-element.50), channel_id=1, source_target_pairs={{0,8},{16,24},{32,40},{48,56},{1,9},{17,25},{33,41},{49,57},{2,10}... | collective-permute-start | bytes 884744 | tf_op jit(solution)/shard_map/ppermute | solution.py:519
  71.0 6.1 %collective-permute-start.11 = (f32[72,1024]{1,0:T(8,128)S(1)}, f32[72,1024]{1,0:T(8,128)S(1)}, u32[]{:S(2)}, u32[]{:S(2)}) collective-permute-start(f32[72,1024]{1,0:T(8,128)S(1)} %get-tuple-element.52), channel_id=1, source_target_pairs={{8,16},{24,32},{40,48},{56,1},{9,17},{25,33},{41,49},{57,2},{10,18... | collective-permute-start | bytes 884744 | tf_op jit(solution)/shard_map/ppermute | solution.py:519
  78.8 21.7 %collective-permute-start.14 = (f32[40,1024]{1,0:T(8,128)S(1)}, f32[40,1024]{1,0:T(8,128)S(1)}, u32[]{:S(2)}, u32[]{:S(2)}) collective-permute-start(f32[40,1024]{1,0:T(8,128)S(1)} %get-tuple-element.57), channel_id=1, source_target_pairs={{0,8},{16,24},{32,40},{48,56},{1,9},{17,25},{33,41},{49,57},{2,10}... | collective-permute-start | bytes 491528 | tf_op jit(solution)/shard_map/ppermute | solution.py:519
  85.6 14.9 %collective-permute-start.16 = (f32[40,1024]{1,0:T(8,128)S(1)}, f32[40,1024]{1,0:T(8,128)S(1)}, u32[]{:S(2)}, u32[]{:S(2)}) collective-permute-start(f32[40,1024]{1,0:T(8,128)S(1)} %get-tuple-element.59), channel_id=1, source_target_pairs={{8,16},{24,32},{40,48},{56,1},{9,17},{25,33},{41,49},{57,2},{10,18... | collective-permute-start | bytes 491528 | tf_op jit(solution)/shard_map/ppermute | solution.py:519
  87.8 6.2 %collective-permute-start.13 = (f32[24,1024]{1,0:T(8,128)S(1)}, f32[24,1024]{1,0:T(8,128)S(1)}, u32[]{:S(2)}, u32[]{:S(2)}) collective-permute-start(f32[24,1024]{1,0:T(8,128)S(1)} %get-tuple-element.56), channel_id=1, source_target_pairs={{0,8},{16,24},{32,40},{48,56},{1,9},{17,25},{33,41},{49,57},{2,10}... | collective-permute-start | bytes 294920 | tf_op jit(solution)/shard_map/ppermute | solution.py:519
  93.0 4.0 %collective-permute-start.15 = (f32[24,1024]{1,0:T(8,128)S(1)}, f32[24,1024]{1,0:T(8,128)S(1)}, u32[]{:S(2)}, u32[]{:S(2)}) collective-permute-start(f32[24,1024]{1,0:T(8,128)S(1)} %get-tuple-element.58), channel_id=1, source_target_pairs={{8,16},{24,32},{40,48},{56,1},{9,17},{25,33},{41,49},{57,2},{10,18... | collective-permute-start | bytes 294920 | tf_op jit(solution)/shard_map/ppermute | solution.py:519
  98.7 8.4 %collective-permute-start.17 = (f32[2,4,24,128]{3,2,1,0:T(8,128)S(1)}, f32[2,4,24,128]{3,2,1,0:T(8,128)S(1)}, u32[]{:S(2)}, u32[]{:S(2)}) collective-permute-start(f32[2,4,24,128]{3,2,1,0:T(8,128)S(1)} %get-tuple-element.63), channel_id=1, source_target_pairs={{0,16},{8,24},{16,0},{24,8},{32,48},{40,56},{48,32},{56,40},{1,17}... | collective-permute-start | bytes 294920 | tf_op jit(solution)/shard_map/ppermute | solution.py:484
  103.2 25.3 %collective-permute-start.20 = (f32[2,4,40,128]{3,2,1,0:T(8,128)S(1)}, f32[2,4,40,128]{3,2,1,0:T(8,128)S(1)}, u32[]{:S(2)}, u32[]{:S(2)}) collective-permute-start(f32[2,4,40,128]{3,2,1,0:T(8,128)S(1)} %get-tuple-element.67), channel_id=1, source_target_pairs={{0,16},{8,24},{16,0},{24,8},{32,48},{40,56},{48,32},{56,40},{1,17}... | collective-permute-start | bytes 491528 | tf_op jit(solution)/shard_map/ppermute | solution.py:484
  104.7 23.7 %collective-permute-start.21 = (f32[2,4,40,128]{3,2,1,0:T(8,128)S(1)}, f32[2,4,40,128]{3,2,1,0:T(8,128)S(1)}, u32[]{:S(2)}, u32[]{:S(2)}) collective-permute-start(f32[2,4,40,128]{3,2,1,0:T(8,128)S(1)} %get-tuple-element.68), channel_id=1, source_target_pairs={{0,32},{8,40},{16,48},{24,56},{32,0},{40,8},{48,16},{56,24},{1,33}... | collective-permute-start | bytes 491528 | tf_op jit(solution)/shard_map/ppermute | solution.py:484
  104.7 23.7 %collective-permute-start.22 = (f32[2,4,40,128]{3,2,1,0:T(8,128)S(1)}, f32[2,4,40,128]{3,2,1,0:T(8,128)S(1)}, u32[]{:S(2)}, u32[]{:S(2)}) collective-permute-start(f32[2,4,40,128]{3,2,1,0:T(8,128)S(1)} %get-tuple-element.69), channel_id=1, source_target_pairs={{0,48},{8,56},{16,32},{24,40},{32,16},{40,24},{48,0},{56,8},{1,49}... | collective-permute-start | bytes 491528 | tf_op jit(solution)/shard_map/ppermute | solution.py:484
  106.9 21.5 %collective-permute-start.18 = (f32[2,4,24,128]{3,2,1,0:T(8,128)S(1)}, f32[2,4,24,128]{3,2,1,0:T(8,128)S(1)}, u32[]{:S(2)}, u32[]{:S(2)}) collective-permute-start(f32[2,4,24,128]{3,2,1,0:T(8,128)S(1)} %get-tuple-element.64), channel_id=1, source_target_pairs={{0,32},{8,40},{16,48},{24,56},{32,0},{40,8},{48,16},{56,24},{1,33}... | collective-permute-start | bytes 294920 | tf_op jit(solution)/shard_map/ppermute | solution.py:484
  107.1 21.3 %collective-permute-start.19 = (f32[2,4,24,128]{3,2,1,0:T(8,128)S(1)}, f32[2,4,24,128]{3,2,1,0:T(8,128)S(1)}, u32[]{:S(2)}, u32[]{:S(2)}) collective-permute-start(f32[2,4,24,128]{3,2,1,0:T(8,128)S(1)} %get-tuple-element.65), channel_id=1, source_target_pairs={{0,48},{8,56},{16,32},{24,40},{32,16},{40,24},{48,0},{56,8},{1,49}... | collective-permute-start | bytes 294920 | tf_op jit(solution)/shard_map/ppermute | solution.py:484
  128.5 18.7 %collective-permute-start.23 = (f32[4,4,64,128]{3,2,1,0:T(8,128)S(1)}, f32[4,4,64,128]{3,2,1,0:T(8,128)S(1)}, u32[]{:S(2)}, u32[]{:S(2)}) collective-permute-start(f32[4,4,64,128]{3,2,1,0:T(8,128)S(1)} %pass_on.1), channel_id=1, source_target_pairs={{0,8},{8,0},{16,24},{24,16},{32,40},{40,32},{48,56},{56,48},{1,9},... | collective-permute-start | bytes 1572872 | tf_op jit(solution)/shard_map/ppermute | solution.py:558
